TPU v7x, 128 devices: a whole 4x4x4 slice. The times are simulated.
128 devices in a mesh: gx: 8 (over x, core), gy: 16 (over z, y).
Axes of the slice: x: 4, y: 4, z: 4, core: 2. Of those that a mesh axis runs over, the one named last changes fastest.
Arguments:
- weights: float32 [2, 64, 16, 32, 512], P(None, None, 'gx', 'gy'), may hold values from -6 to 6
- interp: float32 [4, 4, 64, 64], replicated, may hold values from -0.375 to 0.375
- travel: float32 [64, 4096], replicated, may hold values from -3.140625 to 3.140625
- entry_rows: int32 [3, 8, 16, 2048], P(None, 'gx', 'gy'), may hold values from 0 to 4095
- exit_rows: int32 [3, 8, 16, 2048], P(None, 'gx', 'gy'), may hold values from 0 to 4095
Outputs:
- result: float32 [2, 64, 2, 4, 32768], P(None, None, None, None, ('gx', 'gy'))
All inputs are finite; a program needn't handle non-finite values.
Results may differ from a plain program's by a relative error of at most 0.0001.
Values sent between devices are 32-bit elements; how exact they have to be, the bound alone decides.
No kernel may reach another device: no remote copies, remote signals or barrier semaphores. Data moves between devices by JAX's collectives and lax.ppermute only.
A program may use at most 128 MiB of HBM per device.

v0:
```python
import jax
import jax.numpy as jnp
from jax import lax
from jax.sharding import PartitionSpec as P

highest = lax.Precision.HIGHEST


def from_partner(x, axis, distance):
    return lax.ppermute(x, axis, [(i, i ^ 1 << distance) for i in range(lax.axis_size(axis))])


def rotate(fields, travel, row_index, sign):
    angles = jnp.take(travel, row_index, axis=1)
    cos_part = jnp.cos(angles)
    sin_part = jnp.sin(angles) * sign
    real_part = fields[0]
    imag_part = fields[1]
    return jnp.stack(
        [cos_part * real_part - sin_part * imag_part, sin_part * real_part + cos_part * imag_part]
    )


def shards(weights, interp, travel, entry_rows, exit_rows):
    count = weights.shape[-1]
    points = interp.shape[-1]
    x_size = lax.axis_size("gx")
    y_size = lax.axis_size("gy")
    fields = weights.reshape(2, points, 4 * count)
    fields = rotate(fields, travel, entry_rows[0, 0, 0], -1.0)
    merged = jnp.einsum(
        "kcts,rsca->rtka", interp, fields.reshape(2, points, 4, count), precision=highest
    )
    fields = rotate(merged.reshape(2, points, 4 * count), travel, exit_rows[0, 0, 0], 1.0)
    for section in (1, 2):
        level_bit = section - 1
        x_bit = lax.axis_index("gx") >> level_bit & 1
        y_bit = lax.axis_index("gy") >> level_bit & 1
        fields = rotate(fields, travel, entry_rows[section, 0, 0], -1.0)
        target_child = 2 * x_bit + y_bit
        matrices = lax.dynamic_index_in_dim(interp, target_child, axis=0, keepdims=False)
        paired = jnp.stack([fields, from_partner(fields, "gy", level_bit)])
        crossed = from_partner(paired, "gx", level_bit)
        sources = jnp.concatenate([paired, crossed], axis=0)
        children = jnp.stack(
            [
                target_child,
                2 * x_bit + 1 - y_bit,
                2 * (1 - x_bit) + y_bit,
                2 * (1 - x_bit) + 1 - y_bit,
            ]
        )
        chosen = jnp.take(matrices, children, axis=0)
        fields = jnp.einsum("qts,qrsp->rtp", chosen, sources, precision=highest)
        fields = rotate(fields, travel, exit_rows[section, 0, 0], 1.0)
    moved = lax.all_to_all(
        fields.reshape(2, points, 4, x_size * y_size, -1),
        ("gx", "gy"),
        split_axis=3,
        concat_axis=3,
        tiled=True,
    )
    moved = moved.reshape(2, points, 4, x_size // 4, 2, 2, y_size // 4, 2, 2, -1)
    moved = moved.transpose(0, 1, 3, 6, 9, 2, 5, 8, 4, 7)
    return moved.reshape(2, points, x_size // 4, y_size // 4, -1)


def solution(mesh):
    return jax.shard_map(
        shards,
        mesh=mesh,
        in_specs=(
            P(None, None, "gx", "gy", None),
            P(),
            P(),
            P(None, "gx", "gy", None),
            P(None, "gx", "gy", None),
        ),
        out_specs=P(None, None, None, None, ("gx", "gy")),
        check_vma=False,
    )
```

profile of v0, /device:TPU:1, one launch (start us, length us, event | category | flops | bytes accessed | tf_op | source)
XLA Modules:
  0.0 229.7 jit_solution(8087532263155459867)
XLA Ops:
  0.0 0.7 fusion.48
  0.8 0.7 fusion.47
  1.5 1.6 fusion.46
  3.2 1.3 squeeze.55
  4.4 1.2 squeeze.56
  5.7 0.6 copy.45
  6.3 5.5 %gather_fusion.5 = f32[2048,64]{1,0:T(8,128)S(1)} fusion(f32[64,4096]{0,1:T(8,128)S(1)} %copy.45, s32[2048]{0:T(1024)S(1)} %fusion.37), kind=kCustom, calls=%fused_computation.6.clone | custom fusion | bytes 1056768 | tf_op jit(solution)/shard_map/jit(_take)/gather | solution.py:14
  11.8 1.1 copy.56
  12.9 3.8 %multiply_subtract_fusion.3 = (f32[64,2048]{1,0:T(8,128)S(1)}, f32[64,2048]{1,0:T(8,128)}) fusion(f32[64,2048]{1,0:T(8,128)} %squeeze.56, f32[64,2048]{1,0:T(8,128)} %squeeze.55, f32[2048,64]{0,1:T(8,128)} %copy.56, pred[2048]{0:T(1024)(128)(4,1)S(1)} %compare_and_fusion), kind=kLoop, calls=%fused_computation.62 | loop fusion | flops 1048576 | bytes 2623488 | tf_op jit(solution)/shard_map/sub | solution.py:20
  17.2 1.4 stack.85
  18.8 2.2 convolution_bitcast_fusion
  21.4 1.0 copy.72
  22.7 1.0 copy.73
  23.7 5.5 %gather_fusion.4 = f32[2048,64]{1,0:T(8,128)S(1)} fusion(f32[64,4096]{0,1:T(8,128)S(1)} %copy.45, s32[2048]{0:T(1024)S(1)} %fusion.36), kind=kCustom, calls=%fused_computation.5.clone | custom fusion | bytes 1056768 | tf_op jit(solution)/shard_map/jit(_take)/gather | solution.py:14
  29.1 1.1 copy.54
  30.3 7.6 %gather_fusion.3 = f32[2048,64]{1,0:T(8,128)} fusion(f32[64,4096]{0,1:T(8,128)S(1)} %copy.45, s32[2048]{0:T(1024)S(1)} %fusion.35), kind=kCustom, calls=%fused_computation.4.clone | custom fusion | bytes 1056768 | tf_op jit(solution)/shard_map/jit(_take)/gather | solution.py:14
  37.9 1.5 copy.52
  39.4 4.9 %subtract_bitcast_fusion.1 = (f32[1,64,2048]{2,1,0:T(8,128)S(1)}, f32[64,2048]{1,0:T(8,128)S(1)}, f32[64,2048]{1,0:T(8,128)S(1)}) fusion(f32[2048,64]{0,1:T(8,128)S(1)} %copy.52, pred[2048]{0:T(1024)(128)(4,1)S(1)} %get-tuple-element.38, f32[64,2048]{1,0:T(8,128)} %bitcast.191, f32[64,2048]{1,0:T(8,128)} %bitcast.190, f32[2048,64]{0,1:T(8,128)S(1)} %copy-done.2, ...), kind=kLoop, calls=%fused_computation.58 | loop fusion | flops 1572864 | bytes 3674112 | tf_op jit(solution)/shard_map/stack | solution.py:19
  44.4 2.0 add_bitcast_fusion.1
  46.6 2.2 collective-permute-start
  48.8 22.5 %collective-permute-done = f32[2,64,2048]{2,1,0:T(8,128)S(1)} collective-permute-done((f32[2,64,2048]{2,1,0:T(8,128)S(1)}, f32[2,64,2048]{2,1,0:T(8,128)S(1)}, u32[]{:S(2)}, u32[]{:S(2)}) %collective-permute-start) | collective-permute-done | bytes 1048608 | tf_op jit(solution)/shard_map/ppermute | solution.py:10
  71.3 1.6 pad_maximum_fusion
  72.9 1.6 collective-permute-start.1
  74.5 5.5 %gather_fusion.2 = f32[2048,64]{1,0:T(8,128)S(1)} fusion(f32[64,4096]{0,1:T(8,128)S(1)} %copy.45, s32[2048]{0:T(1024)S(1)} %fusion.34), kind=kCustom, calls=%fused_computation.3.clone | custom fusion | bytes 1056768 | tf_op jit(solution)/shard_map/jit(_take)/gather | solution.py:14
  80.0 1.1 copy.50
  81.1 7.6 %gather_fusion.1 = f32[2048,64]{1,0:T(8,128)} fusion(f32[64,4096]{0,1:T(8,128)S(1)} %copy.45, s32[2048]{0:T(1024)S(1)} %fusion.33), kind=kCustom, calls=%fused_computation.2.clone | custom fusion | bytes 1056768 | tf_op jit(solution)/shard_map/jit(_take)/gather | solution.py:14
  88.8 1.5 copy.48
  90.4 0.6 gather_fusion.6
  91.0 4.6 %fusion.15 = f32[2,64,2048]{2,1,0:T(8,128)S(1)} fusion(f32[2,2,64,2048]{3,2,0,1:T(8,128)} %collective-permute-done.1, f32[1,2,64,2048]{3,2,0,1:T(8,128)} %bitcast.193, f32[1,2,64,2048]{3,2,0,1:T(8,128)} %copy-done, f32[4,64,64]{2,1,0:T(8,128)S(1)} %gather_fusion.6, pred[4]{0:T(512)(128)(4,1)S(1)} %get-tuple-element.12), kind=kOutput, calls=%fused_computation.21 | convolution fusion | flops 807419904 | bytes 5308420 | tf_op jit(solution)/shard_map/qts,qrsp->rtp/dot_general | solution.py:54
  95.7 3.9 %subtract_bitcast_fusion = (f32[1,64,2048]{2,1,0:T(8,128)S(1)}, f32[64,2048]{1,0:T(8,128)S(1)}, f32[64,2048]{1,0:T(8,128)S(1)}) fusion(f32[2048,64]{0,1:T(8,128)S(1)} %copy.48, pred[2048]{0:T(1024)(128)(4,1)S(1)} %get-tuple-element.40, f32[2,64,2048]{2,1,0:T(8,128)S(1)} %fusion.15, f32[2048,64]{0,1:T(8,128)S(1)} %copy-done.1, ...), kind=kLoop, calls=%fused_computation.54 | loop fusion | flops 1572864 | bytes 3674112 | tf_op jit(solution)/shard_map/stack | solution.py:19
  99.6 2.0 add_bitcast_fusion
  101.9 3.2 %collective-permute-start.2 = (f32[2,64,2048]{2,1,0:T(8,128)S(1)}, f32[2,64,2048]{2,1,0:T(8,128)S(1)}, u32[]{:S(2)}, u32[]{:S(2)}) collective-permute-start(f32[2,64,2048]{2,1,0:T(8,128)S(1)} %get-tuple-element.22), channel_id=1, source_target_pairs={{0,2},{1,3},{2,0},{3,1},{4,6},{5,7},{6,4},{7,5},{8,10},{9,11},{10,... | collective-permute-start | bytes 3145736 | tf_op jit(solution)/shard_map/ppermute | solution.py:10
  105.1 23.4 %collective-permute-done.2 = f32[2,64,2048]{2,1,0:T(8,128)S(1)} collective-permute-done((f32[2,64,2048]{2,1,0:T(8,128)S(1)}, f32[2,64,2048]{2,1,0:T(8,128)S(1)}, u32[]{:S(2)}, u32[]{:S(2)}) %collective-permute-start.2) | collective-permute-done | bytes 1048608 | tf_op jit(solution)/shard_map/ppermute | solution.py:10
  128.4 1.7 pad_maximum_fusion.1
  130.1 1.1 collective-permute-start.3
  131.2 7.6 %gather_fusion = f32[2048,64]{1,0:T(8,128)} fusion(f32[64,4096]{0,1:T(8,128)S(1)} %copy.45, s32[2048]{0:T(1024)S(1)} %fusion.32), kind=kCustom, calls=%fused_computation.clone | custom fusion | bytes 1056768 | tf_op jit(solution)/shard_map/jit(_take)/gather | solution.py:14
  138.8 1.5 copy.46
  141.0 35.8 %collective-permute-done.3 = f32[2,2,64,2048]{3,2,1,0:T(8,128)} collective-permute-done((f32[2,2,64,2048]{3,2,1,0:T(8,128)}, f32[2,2,64,2048]{3,2,1,0:T(8,128)}, u32[]{:S(2)}, u32[]{:S(2)}) %collective-permute-start.3) | collective-permute-done | bytes 2097184 | tf_op jit(solution)/shard_map/ppermute | solution.py:10
  176.8 4.4 %fusion.12 = f32[2,64,2048]{2,1,0:T(8,128)S(1)} fusion(f32[2,2,64,2048]{3,2,1,0:T(8,128)} %collective-permute-done.3, f32[1,2,64,2048]{3,2,1,0:T(8,128)} %bitcast.195, f32[1,2,64,2048]{3,2,1,0:T(8,128)S(1)} %get-tuple-element.21, f32[4,64,64]{2,1,0:T(8,128)S(1)} %gather_fusion.7, pred[4]{0:T(512)(128)(4,1)S(1)} %get-tuple-element.6), kind=kOutput, calls=%fused_computation.20 | convolution fusion | flops 807419904 | bytes 5308420 | tf_op jit(solution)/shard_map/qts,qrsp->rtp/dot_general | solution.py:54
  181.3 2.1 multiply_subtract_fusion
  183.7 1.3 copy.64
  185.0 1.8 copy_bitcast_fusion
  186.8 1.9 reshape.133
  188.7 30.3 %all_to_all.5 = f32[128,1,2048]{2,1,0:T(1,128)S(1)} all-to-all(f32[128,1,2048]{2,1,0:T(1,128)S(1)} %reshape.133), channel_id=1, replica_groups=mesh['gx'=8,'gy'=16] {'gx','gy'}, dimensions={0} | all-to-all | bytes 2097152 | tf_op jit(solution)/shard_map/all_to_all | solution.py:56
  219.5 3.1 %reduce = f32[128,2048]{1,0:T(8,128)S(1)} reduce(f32[128,1,2048]{2,1,0:T(1,128)S(1)} %all_to_all.5, f32[]{:T(128)} %broadcast.141), dimensions={1}, to_apply=%all_to_all.3.reduce_sub_computation | reduce | bytes 2097156 | tf_op jit(solution)/shard_map/all_to_all | solution.py:56
  222.6 1.4 reshape.134
  224.1 3.0 %copy.66 = f32[2,64,4,2,2,2,4,2,2,4]{1,7,4,8,5,2,9,6,3,0:T(2,128)} copy(f32[2,64,4,2,2,2,4,2,2,4]{1,9,2,0,8,7,6,5,4,3:T(4,128)S(1)} %bitcast.184) | data formatting | bytes 2097152 | tf_op jit(solution)/shard_map/reshape | solution.py:63
  227.0 2.7 %copy.67 = f32[2,64,2,4,256]{4,3,2,1,0:T(4,128)} copy(f32[2,64,2,4,256]{1,4,3,2,0:T(8,128)} %bitcast.185) | data formatting | bytes 2097152 | tf_op jit(solution)/shard_map/reshape | solution.py:65
  (41 shorter events, 3.6 us)
Async XLA Ops:
  1.5 4.2 %copy-start.4 = (f32[64,4096]{1,0:T(8,128)S(1)}, f32[64,4096]{1,0:T(8,128)}, u32[]{:S(2)}) copy-start(f32[64,4096]{1,0:T(8,128)} %param.11) | copy-start | bytes 3145732
  30.2 9.2 %copy-start.2 = (f32[2048,64]{0,1:T(8,128)S(1)}, f32[2048,64]{0,1:T(8,128)}, u32[]{:S(2)}) copy-start(f32[2048,64]{0,1:T(8,128)} %copy.54) | copy-start | bytes 1572868
  46.5 26.3 %copy-start = (f32[1,2,64,2048]{3,2,0,1:T(8,128)}, f32[1,2,64,2048]{3,2,0,1:T(8,128)S(1)}, u32[]{:S(2)}) copy-start(f32[1,2,64,2048]{3,2,0,1:T(8,128)S(1)} %get-tuple-element.23) | copy-start | bytes 3145732
  46.6 24.7 %collective-permute-start = (f32[2,64,2048]{2,1,0:T(8,128)S(1)}, f32[2,64,2048]{2,1,0:T(8,128)S(1)}, u32[]{:S(2)}, u32[]{:S(2)}) collective-permute-start(f32[2,64,2048]{2,1,0:T(8,128)S(1)} %get-tuple-element.24), channel_id=1, source_target_pairs={{0,1},{1,0},{2,3},{3,2},{4,5},{5,4},{6,7},{7,6},{8,9},{9,8},{10,11... | collective-permute-start | bytes 3145736 | tf_op jit(solution)/shard_map/ppermute | solution.py:10
  71.3 1.7 copy-start.5
  72.9 18.1 %collective-permute-start.1 = (f32[2,2,64,2048]{3,2,0,1:T(8,128)}, f32[2,2,64,2048]{3,2,0,1:T(8,128)}, u32[]{:S(2)}, u32[]{:S(2)}) collective-permute-start(f32[2,2,64,2048]{3,2,0,1:T(8,128)} %pad_maximum_fusion), channel_id=1, source_target_pairs={{0,16},{16,0},{32,48},{48,32},{64,80},{80,64},{96,112},{112,96},{1... | collective-permute-start | bytes 6291464 | tf_op jit(solution)/shard_map/ppermute | solution.py:10
  81.1 9.3 %copy-start.3 = (f32[4,4,64,64]{3,2,1,0:T(8,128)S(1)}, f32[4,4,64,64]{3,2,1,0:T(8,128)}, u32[]{:S(2)}) copy-start(f32[4,4,64,64]{3,2,1,0:T(8,128)} %param.10) | copy-start | bytes 786436
  91.0 4.7 %copy-start.1 = (f32[2048,64]{0,1:T(8,128)S(1)}, f32[2048,64]{0,1:T(8,128)}, u32[]{:S(2)}) copy-start(f32[2048,64]{0,1:T(8,128)} %copy.50) | copy-start | bytes 1572868
  101.9 26.5 %collective-permute-start.2 = (f32[2,64,2048]{2,1,0:T(8,128)S(1)}, f32[2,64,2048]{2,1,0:T(8,128)S(1)}, u32[]{:S(2)}, u32[]{:S(2)}) collective-permute-start(f32[2,64,2048]{2,1,0:T(8,128)S(1)} %get-tuple-element.22), channel_id=1, source_target_pairs={{0,2},{1,3},{2,0},{3,1},{4,6},{5,7},{6,4},{7,5},{8,10},{9,11},{10,... | collective-permute-start | bytes 3145736 | tf_op jit(solution)/shard_map/ppermute | solution.py:10
  128.4 1.7 copy-start.6
  130.1 46.7 %collective-permute-start.3 = (f32[2,2,64,2048]{3,2,1,0:T(8,128)}, f32[2,2,64,2048]{3,2,1,0:T(8,128)}, u32[]{:S(2)}, u32[]{:S(2)}) collective-permute-start(f32[2,2,64,2048]{3,2,1,0:T(8,128)} %pad_maximum_fusion.1), channel_id=1, source_target_pairs={{0,32},{16,48},{32,0},{48,16},{64,96},{80,112},{96,64},{112,80},{1... | collective-permute-start | bytes 6291464 | tf_op jit(solution)/shard_map/ppermute | solution.py:10
where the time goes:
time: 230 us
  waiting for transfers between devices  81.7 us (36%)
  local copies, waits for them, and re-layouts  70.5 us (31%)
  blocking collectives  30.3 us (13%)
  other arithmetic  27.5 us (12%)
  matrix products  11.2 us (5%)
  starting transfers between devices  8.07 us (4%)
    ppermute x4, waiting for transfers between devices, from_partner(): lax.ppermute(x, axis, [(i, i ^ 1 << distance) for i in range(lax.axis_siz...  81.7 us
    gather x12, local copies, waits for them, and re-layouts, rotate(): angles = jnp.take(travel, row_index, axis=1)  47.2 us
    all_to_all x1, blocking collectives, shards(): lax.all_to_all(fields.reshape(2, points, 4, x_size * y_size, -1), ('gx',...  30.3 us
    another operation x4, other arithmetic, rotate(): jnp.stack([cos_part * real_part - sin_part * imag_part, sin_part * real_p...  12.9 us
    dot_general x2, matrix products, shards(): fields = jnp.einsum('qts,qrsp->rtp', chosen, sources, precision=highest)  9.05 us
    ppermute x4, starting transfers between devices, from_partner(): lax.ppermute(x, axis, [(i, i ^ 1 << distance) for i in range(lax.axis_siz...  8.07 us
    unnamed x19, local copies, waits for them, and re-layouts  5.96 us
    sub x2, other arithmetic, rotate(): cos_part * real_part - sin_part * imag_part  5.85 us
  transfers between devices with their start and end apart: 4, of which 3 were waited for; matrix products, arithmetic and copies ran while one was open for 11% of the time, Pallas kernels for 0%

commit v1 on v0

v1 whole, which is shorter than its diff:
```python
import jax
import jax.numpy as jnp
from jax import lax
from jax.sharding import PartitionSpec as P

high = lax.Precision.HIGH


def rotate(fields, angles):
    cos_part = jnp.cos(angles)
    sin_part = jnp.sin(angles)
    return jnp.stack(
        [
            cos_part * fields[0] - sin_part * fields[1],
            sin_part * fields[0] + cos_part * fields[1],
        ]
    )


def shards(weights, interp, travel, entry_rows, exit_rows):
    count = weights.shape[-1]
    points = interp.shape[-1]
    devices = lax.axis_size("gx") * lax.axis_size("gy")
    own = count // devices
    look = lambda rows: jnp.take(travel, rows, axis=1)
    matrix = interp.transpose(0, 2, 1, 3).reshape(4 * points, 4 * points)
    fields = weights.reshape(2, points, 4 * count)
    fields = rotate(fields, -look(entry_rows[0, 0, 0]))
    fields = jnp.einsum(
        "kcts,rsca->rtka", interp, fields.reshape(2, points, 4, count), precision=high
    ).reshape(2, points, 4 * count)
    fields = rotate(fields, look(exit_rows[0, 0, 0]) - look(entry_rows[1, 0, 0]))
    rows = jnp.stack([exit_rows[1, 0, 0], entry_rows[2, 0, 0], exit_rows[2, 0, 0]])
    payload = jnp.concatenate(
        [fields.reshape(2 * points, 4, devices, own), rows.astype(jnp.float32).reshape(3, 4, devices, own)]
    )
    payload = payload.transpose(2, 0, 1, 3).reshape(devices, 1, -1)
    moved = lax.all_to_all(payload, ("gx", "gy"), split_axis=0, concat_axis=0, tiled=True)
    moved = moved.reshape(devices, 2 * points + 3, 4 * own).transpose(1, 2, 0)
    angles = look(moved[2 * points :].astype(jnp.int32).reshape(3, -1))
    fields = moved[: 2 * points].reshape(2, points, 4 * own, 2, 2, 2, 4, 2, 2)
    blocks = interp.reshape(2, 2, 2, 2, points, points)
    fields = jnp.einsum("ijIJts,rsnXaIYbJ->rtnXaiYbj", blocks, fields, precision=high)
    fields = rotate(fields.reshape(2, points, -1), angles[:, 0] - angles[:, 1])
    fields = fields.reshape(2, points, 4 * own, 2, 2, 2, 4, 2, 2)
    fields = jnp.einsum("abABts,rsnXAiYBj->rtnXaiYbj", blocks, fields, precision=high)
    fields = rotate(fields.reshape(2, points, -1), angles[:, 2])
    fields = fields.reshape(2, points, 4, own, 2, 2, 2, 4, 2, 2)
    fields = fields.transpose(0, 1, 4, 7, 3, 2, 6, 9, 5, 8)
    return fields.reshape(2, points, 2, 4, -1)


def solution(mesh):
    return jax.shard_map(
        shards,
        mesh=mesh,
        in_specs=(
            P(None, None, "gx", "gy", None),
            P(),
            P(),
            P(None, "gx", "gy", None),
            P(None, "gx", "gy", None),
        ),
        out_specs=P(None, None, None, None, ("gx", "gy")),
        check_vma=False,
    )
```

time: 230 us -> 167 us (0.73)
  waiting for transfers between devices: 81.7 us -> 0 us
  local copies, waits for them, and re-layouts: 70.5 us -> 94.7 us
  starting transfers between devices: 8.07 us -> 0 us
  other arithmetic: 27.5 us -> 33.6 us
  matrix products: 11.2 us -> 6.24 us
    ppermute x4 -> x0, waiting for transfers between devices: 81.7 us -> none  [from_partner(): lax.ppermute(x, axis, [(i, i ^ 1 << distance) for i in range(lax.axis_siz...]
    another operation x8 -> x2, other arithmetic: 16.5 us -> 4.19 us  [rotate(): jnp.stack([cos_part * fields[0] - sin_part * fields[1], sin_part * fields...]
    cos x0 -> x1, other arithmetic: none -> 8.26 us  [rotate(): cos_part = jnp.cos(angles)]
    ppermute x4 -> x0, starting transfers between devices: 8.07 us -> none  [from_partner(): lax.ppermute(x, axis, [(i, i ^ 1 << distance) for i in range(lax.axis_siz...]
    slice x6 -> x10, local copies, waits for them, and re-layouts: 3.87 us -> 11.7 us  [the longest x5 5.42 us: rotate(): fields[0]]
    another operation x4 -> x9, local copies, waits for them, and re-layouts: 2.09 us -> 8.91 us  [the longest x3 7.79 us: rotate(): jnp.stack([cos_part * fields[0] - sin_part * fields[1], sin_part * fields...]
    sub x2 -> x3, other arithmetic: 5.85 us -> 11.8 us  [rotate(): cos_part * fields[0] - sin_part * fields[1]]
    reshape x2 -> x5, local copies, waits for them, and re-layouts: 5.67 us -> 11.4 us  [the longest x1 3.64 us: shards(): fields.reshape(2 * points, 4, devices, own)]
  transfers between devices with their start and end apart: 4 -> 0, of which waited for: 3 -> 0; matrix products, arithmetic and copies ran while one was open for 11% -> 0% of each run, Pallas kernels for 0% -> 0%
where the time goes in v1:
time: 167 us; the launch traced here: 166 us
  local copies, waits for them, and re-layouts  94.7 us (57%)
  other arithmetic  33.6 us (20%)
  blocking collectives  31.1 us (19%)
  matrix products  6.24 us (4%)
    gather x6, local copies, waits for them, and re-layouts, shards(): look = lambda rows: jnp.take(travel, rows, axis=1)  47.7 us
    all_to_all x1, blocking collectives, shards(): lax.all_to_all(payload, ('gx', 'gy'), split_axis=0, concat_axis=0, tiled=...  31.1 us
    sub x3, other arithmetic, rotate(): cos_part * fields[0] - sin_part * fields[1]  11.8 us
    cos x1, other arithmetic, rotate(): cos_part = jnp.cos(angles)  8.26 us
    another operation x3, local copies, waits for them, and re-layouts, rotate(): jnp.stack([cos_part * fields[0] - sin_part * fields[1], sin_part * fields...  7.79 us
    slice x5, local copies, waits for them, and re-layouts, rotate(): fields[0]  5.42 us
    unnamed x15, local copies, waits for them, and re-layouts  4.97 us
    another operation x2, other arithmetic, rotate(): jnp.stack([cos_part * fields[0] - sin_part * fields[1], sin_part * fields...  4.19 us

profile of v1, /device:TPU:1, one launch (start us, length us, event | category | flops | bytes accessed | tf_op | source)
XLA Modules:
  0.0 166.0 jit_solution(5229356244092159677)
XLA Ops:
  0.0 0.9 slice_reduce_fusion.2
  1.0 1.8 %copy.122 = f32[64,4096]{0,1:T(8,128)S(1)} copy(f32[64,4096]{1,0:T(8,128)} %param.9) | data formatting | bytes 2097152 | tf_op args[2]
  2.8 2.4 %fusion.28 = (f32[1,64,2,2,512]{4,3,2,1,0:T(2,128)}, f32[1,64,2,2,512]{4,3,2,1,0:T(2,128)S(1)}) fusion(f32[2,64,2,2,512]{4,3,2,1,0:T(2,128)} %param.7), kind=kLoop, calls=%fused_computation.65 | loop fusion | bytes 2097152 | tf_op jit(solution)/shard_map/slice | solution.py:14
  5.2 2.4 %copy.127 = f32[1,64,2,2,512]{1,4,3,2,0:T(8,128)} copy(f32[1,64,2,2,512]{4,3,2,1,0:T(2,128)} %get-tuple-element.26) | data formatting | bytes 1048576 | tf_op jit(solution)/shard_map/slice | solution.py:14
  7.5 1.3 copy.128
  8.9 7.6 %gather_fusion.3 = f32[2048,64]{1,0:T(8,128)} fusion(f32[64,4096]{0,1:T(8,128)S(1)} %copy.122, s32[2048]{0:T(1024)S(1)} %fusion.23), kind=kCustom, calls=%fused_computation.2.clone | custom fusion | bytes 1056768 | tf_op jit(solution)/shard_map/jit(_take)/gather | solution.py:25
  16.4 8.3 %fusion.12 = (f32[64,2048]{0,1:T(8,128)}, f32[64,2048]{0,1:T(8,128)}) fusion(f32[1,64,2,2,512]{1,4,3,2,0:T(8,128)} %copy.128, f32[1,64,2,2,512]{1,4,3,2,0:T(8,128)} %copy.127, f32[2048,64]{1,0:T(8,128)} %gather_fusion.3, pred[2048]{0:T(1024)(128)(4,1)S(1)} %compare_and_fusion.1), kind=kLoop, calls=%fused_computation.22 | loop fusion | flops 1048576 | bytes 2623488 | tf_op jit(solution)/shard_map/sub | solution.py:14
  24.7 1.5 copy.131
  26.3 2.3 %copy.132 = f32[1,64,4,512]{3,1,2,0:T(8,128)} copy(f32[1,64,4,512]{1,3,2,0:T(8,128)} %bitcast.146) | data formatting | bytes 1048576 | tf_op jit(solution)/shard_map/stack | solution.py:12
  28.6 1.7 %convolution_bitcast_fusion = f32[2,64,4,512]{3,1,2,0:T(8,128)S(1)} fusion(f32[1,64,4,512]{3,1,2,0:T(8,128)} %copy.132, f32[1,64,4,512]{3,1,2,0:T(8,128)S(1)} %copy.131, f32[4,4,64,64]{3,2,1,0:T(8,128)S(1)} %copy-done), kind=kOutput, calls=%fused_computation.14 | convolution fusion | flops 402915328 | bytes 2359296 | tf_op jit(solution)/shard_map/kcts,rsca->rtka/dot_general | solution.py:29
  30.4 0.3 copy.133
  30.7 1.0 copy.172
  31.7 0.3 copy.134
  32.0 1.0 copy.173
  33.0 7.6 %gather_fusion.1 = f32[2048,64]{1,0:T(8,128)} fusion(f32[64,4096]{0,1:T(8,128)S(1)} %copy.122, s32[2048]{0:T(1024)S(1)} %fusion.21), kind=kCustom, calls=%fused_computation.clone | custom fusion | bytes 1056768 | tf_op jit(solution)/shard_map/jit(_take)/gather | solution.py:25
  40.6 1.5 copy.123
  42.1 7.6 %gather_fusion.2 = f32[2048,64]{1,0:T(8,128)} fusion(f32[64,4096]{0,1:T(8,128)S(1)} %copy.122, s32[2048]{0:T(1024)S(1)} %fusion.22), kind=kCustom, calls=%fused_computation.1.clone | custom fusion | bytes 1056768 | tf_op jit(solution)/shard_map/jit(_take)/gather | solution.py:25
  49.8 2.4 %copy.125 = f32[2048,64]{0,1:T(8,128)} copy(f32[2048,64]{1,0:T(8,128)} %gather_fusion.2) | data formatting | bytes 1048576 | tf_op jit(solution)/shard_map/jit(_take)/gather | solution.py:25
  52.1 3.1 %subtract_bitcast_fusion = (f32[1,64,2048]{2,1,0:T(8,128)S(1)}, f32[1,64,2048]{2,1,0:T(8,128)S(1)}) fusion(f32[64,2048]{1,0:T(8,128)} %bitcast.157, f32[64,2048]{1,0:T(8,128)} %bitcast.156, f32[2048,64]{0,1:T(8,128)} %copy.125, pred[2048]{0:T(1024)(128)(4,1)S(1)} %compare_and_fusion.2, f32[2048,64]{0,1:T(8,128)S(1)} %copy.123, ...), kind=kLoop, calls=%fused_computation.38 | loop fusion | flops 1179648 | bytes 3149824 | tf_op jit(solution)/shard_map/stack | solution.py:12
  55.3 1.1 pad_maximum_fusion
  56.3 3.9 %copy.135 = f32[2,64,2048]{1,0,2:T(2,128)} copy(f32[2,64,2048]{2,1,0:T(8,128)} %pad_maximum_fusion) | data formatting | bytes 2097152 | tf_op jit(solution)/shard_map/stack | solution.py:12
  60.2 3.6 %reshape.222 = f32[128,4,128,4]{0,3,2,1:T(4,128)} reshape(f32[2,64,2048]{1,0,2:T(2,128)} %copy.135) | data formatting | bytes 2097152 | tf_op jit(solution)/shard_map/reshape | solution.py:35
  63.9 0.3 stack.43
  64.3 0.3 stack.44
  64.7 0.3 stack.45
  65.0 1.4 copy.139
  66.4 3.4 %maximum_bitcast_fusion = f32[128,131,4,4]{1,3,0,2:T(4,128)} fusion(f32[3,4,128,4]{0,3,2,1:T(4,128)} %copy.139, f32[128,4,128,4]{0,3,2,1:T(4,128)} %reshape.222), kind=kLoop, calls=%fused_computation.5 | loop fusion | flops 268288 | bytes 2146304 | tf_op jit(solution)/shard_map/transpose | solution.py:37
  69.8 4.0 %copy.140 = f32[128,131,4,4]{0,3,2,1:T(4,128)} copy(f32[128,131,4,4]{1,3,0,2:T(4,128)} %maximum_bitcast_fusion) | data formatting | bytes 2146304 | tf_op jit(solution)/shard_map/transpose | solution.py:37
  73.8 3.6 %copy.141 = f32[128,1,2096]{2,1,0:T(1,128)} copy(f32[128,1,2096]{0,2,1:T(8,128)} %bitcast.143) | data formatting | bytes 2146304 | tf_op jit(solution)/shard_map/reshape | solution.py:37
  77.5 31.1 %all_to_all.5 = f32[128,1,2096]{2,1,0:T(1,128)} all-to-all(f32[128,1,2096]{2,1,0:T(1,128)} %copy.141), channel_id=1, replica_groups=mesh['gx'=8,'gy'=16] {'gx','gy'}, dimensions={0} | all-to-all | bytes 2146304 | tf_op jit(solution)/shard_map/all_to_all | solution.py:38
  108.6 3.6 %copy.142 = f32[128,1,2096]{0,2,1:T(8,128)} copy(f32[128,1,2096]{2,1,0:T(1,128)} %all_to_all.5) | data formatting | bytes 2146304 | tf_op jit(solution)/shard_map/all_to_all | solution.py:38
  112.2 0.7 fusion.25
  112.9 2.3 %slice.106 = f32[128,16,128]{2,1,0:T(8,128)} slice(f32[131,16,128]{2,1,0:T(8,128)} %bitcast.145), slice={[0:128], [0:16], [0:128]} | slice | bytes 2097152 | tf_op jit(solution)/shard_map/slice | solution.py:41
  115.3 20.9 %gather_fusion = f32[6144,64]{1,0:T(8,128)} fusion(f32[64,4096]{0,1:T(8,128)S(1)} %copy.122, s32[6144]{0:T(1024)S(1)} %broadcast_clamp_fusion), kind=kCustom, calls=%fused_computation.3 | custom fusion | bytes 3170304 | tf_op jit(solution)/shard_map/jit(_take)/gather | solution.py:25
  136.2 3.2 %select_bitcast_fusion = f32[64,3,2048]{0,2,1:T(8,128)S(1)} fusion(f32[3,2048,64]{2,1,0:T(8,128)} %bitcast.140, pred[3,2048]{1,0:T(4,128)(4,1)S(1)} %compare_and_fusion), kind=kLoop, calls=%fused_computation.4 | loop fusion | flops 393216 | bytes 3151872 | tf_op jit(solution)/shard_map/jit(_take)/select_n | solution.py:25
  139.4 8.3 %fusion.18 = (f32[64,1,2048]{0,2,1:T(8,128)}, f32[64,1,2048]{0,2,1:T(8,128)}, f32[64,1,2048]{0,2,1:T(8,128)}, f32[64,1,2048]{0,2,1:T(8,128)}) fusion(f32[64,3,2048]{0,2,1:T(8,128)S(1)} %select_bitcast_fusion), kind=kLoop, calls=%fused_computation.40 | loop fusion | flops 131072 | bytes 3670016 | tf_op jit(solution)/shard_map/cos | solution.py:10
  147.7 1.4 copy.144
  149.1 2.5 %reshape.227 = f32[2,64,16,2,2,2,4,2,2]{1,0,8,7,6,5,4,3,2:T(2,128)S(1)} reshape(f32[128,16,128]{0,2,1:T(8,128)} %copy.144) | data formatting | bytes 2097152 | tf_op jit(solution)/shard_map/reshape | solution.py:41
  151.6 2.7 %fusion.4 = f32[2,64,16,2,2,2,4,2,2]{1,2,8,5,7,6,4,3,0:T(8,128)S(1)} fusion(f32[2,2,2,2,64,64,1,1,1,1,1]{5,4,3,2,1,0,10,9,8,7,6:T(8,128)S(1)} %bitcast.138, f32[2,64,16,2,2,2,4,2,2,1,1]{1,0,8,7,6,5,4,3,2,10,9:T(2,128)S(1)} %bitcast.141), kind=kOutput, calls=%fused_computation.12 | convolution fusion | flops 402653184 | bytes 2359296 | tf_op jit(solution)/shard_map/ijIJts,rsnXaIYbJ->rtnXaiYbj/dot_general | solution.py:43
  154.4 1.4 multiply_subtract_fusion.1
  155.8 1.8 %fusion.7 = f32[2,64,16,2,2,2,4,2,2]{1,2,7,4,8,6,5,3,0:T(8,128)S(1)} fusion(f32[2,2,2,2,64,64,1,1,1,1,1]{5,4,3,2,1,0,10,9,8,7,6:T(8,128)S(1)} %bitcast.139, f32[1,64,16,2,2,2,4,2,2]{1,2,8,5,7,6,4,3,0:T(8,128)S(1)} %get-tuple-element.11, f32[1,64,16,2,2,2,4,2,2]{1,2,8,5,7,6,4,3,0:T(8,128)S(1)} %get-tuple-element.10), kind=kOutput, calls=%fused_computation.13 | convolution fusion | flops 402915328 | bytes 2359296 | tf_op jit(solution)/shard_map/abABts,rsnXAiYBj->rtnXaiYbj/dot_general | solution.py:46
  157.7 0.3 fusion.26
  158.0 0.9 copy-done.1
  158.9 0.3 copy-done.2
  159.2 2.0 %multiply_subtract_fusion = (f32[1,64,4,4,2,2,2,4,2,2]{1,9,8,7,6,5,4,3,2,0:T(2,128)S(1)}, f32[1,64,4,4,2,2,2,4,2,2]{1,9,8,7,6,5,4,3,2,0:T(2,128)S(1)}) fusion(f32[1,64,4,4,2,2,2,4,2,2]{1,9,8,7,6,5,4,3,2,0:T(2,128)S(1)} %bitcast.148, f32[1,64,4,4,2,2,2,4,2,2]{1,9,8,7,6,5,4,3,2,0:T(2,128)S(1)} %bitcast.149, ...), kind=kLoop, calls=%fused_computation.28 | loop fusion | flops 786432 | bytes 3145728 | tf_op jit(solution)/shard_map/sub | solution.py:14
  161.3 1.9 %maximum_bitcast_fusion.2 = f32[2,64,2,4,4,4,2,2,2,2]{1,7,9,3,6,8,2,4,5,0:T(2,128)S(1)} fusion(f32[1,64,4,4,2,2,2,4,2,2]{1,9,8,7,6,5,4,3,2,0:T(2,128)S(1)} %get-tuple-element.9, f32[1,64,4,4,2,2,2,4,2,2]{1,9,8,7,6,5,4,3,2,0:T(2,128)S(1)} %get-tuple-element.8), kind=kLoop, calls=%fused_computation.7 | loop fusion | flops 262144 | bytes 2097152 | tf_op jit(solution)/shard_map/transpose | solution.py:49
  163.2 1.1 copy.155
  164.3 1.7 copy.156
  (26 shorter events, 0.6 us)
Async XLA Ops:
  0.0 28.6 %copy-start = (f32[4,4,64,64]{3,2,1,0:T(8,128)S(1)}, f32[4,4,64,64]{3,2,1,0:T(8,128)}, u32[]{:S(2)}) copy-start(f32[4,4,64,64]{3,2,1,0:T(8,128)} %param.8) | copy-start | bytes 786436
  139.4 8.3 %copy-start.3 = (f32[128,16,128]{2,1,0:T(8,128)S(1)}, f32[128,16,128]{2,1,0:T(8,128)}, u32[]{:S(2)}) copy-start(f32[128,16,128]{2,1,0:T(8,128)} %slice.106) | copy-start | bytes 3145732
  151.6 2.8 %copy-start.4 = (f32[64,1,2048]{0,2,1:T(8,128)S(1)}, f32[64,1,2048]{0,2,1:T(8,128)}, u32[]{:S(2)}) copy-start(f32[64,1,2048]{0,2,1:T(8,128)} %get-tuple-element.14) | copy-start | bytes 1572868
  151.6 2.8 %copy-start.5 = (f32[64,1,2048]{0,2,1:T(8,128)S(1)}, f32[64,1,2048]{0,2,1:T(8,128)}, u32[]{:S(2)}) copy-start(f32[64,1,2048]{0,2,1:T(8,128)} %get-tuple-element.15) | copy-start | bytes 1572868
  157.7 1.2 copy-start.1
  157.7 1.5 copy-start.2

commit v2 on v1

v2 whole, which is shorter than its diff:
```python
import jax
import jax.numpy as jnp
from jax import lax
from jax.experimental import pallas as pl
from jax.experimental.pallas import tpu as pltpu
from jax.sharding import PartitionSpec as P

LANES = 128
HALF = 64
CHUNK = 17
VMEM = pl.BlockSpec(memory_space=pltpu.VMEM)
SMEM = pl.BlockSpec(memory_space=pltpu.SMEM)


def cos_sin(x):
    turns = jnp.floor(x * 0.6366197723675814 + 0.5)
    r = x - turns * 1.5703125
    r = r - turns * 4.837512969970703e-4
    r = r - turns * 7.549789948768648e-8
    z = r * r
    s = r + r * z * ((-1.9515295891e-4 * z + 8.3321608736e-3) * z - 1.6666654611e-1)
    c = 1.0 - 0.5 * z + z * z * (
        (2.443315711809948e-5 * z - 1.388731625493765e-3) * z + 4.166664568298827e-2
    )
    q = turns.astype(jnp.int32)
    odd = (q & 1) == 1
    cos_part = jnp.where(odd, s, c)
    sin_part = jnp.where(odd, c, s)
    cos_part = jnp.where(((q + 1) & 2) == 2, -cos_part, cos_part)
    sin_part = jnp.where((q & 2) == 2, -sin_part, sin_part)
    return cos_part, sin_part


def swap(x):
    return pltpu.roll(x, HALF, 1)


def turn(state, wave, sign):
    low = lax.broadcasted_iota(jnp.int32, state.shape, 1) < HALF
    other = swap(wave)
    cos_part = jnp.where(low, wave, other)
    sin_part = jnp.where(low, other, wave)
    if sign > 0:
        sin_part = jnp.where(low, -sin_part, sin_part)
    else:
        sin_part = jnp.where(low, sin_part, -sin_part)
    return cos_part * state + sin_part * swap(state)


def split(x):
    high = x.astype(jnp.bfloat16)
    low = (x - high.astype(jnp.float32)).astype(jnp.bfloat16)
    return high, low


def product(x, high_ref, low_ref):
    dims = (((1,), (1,)), ((), ()))
    dot = lambda a, b: lax.dot_general(a, b, dims, preferred_element_type=jnp.float32)
    high, low = split(x)
    return dot(high, high_ref[...]) + (dot(high, low_ref[...]) + dot(low, high_ref[...]))


def gather(table, index, out, count, unroll):
    def body(step, carry):
        for n in range(unroll):
            at = step * unroll + n
            out[pl.ds(at, 1), :] = table[pl.ds(index(at), 1), :]
        return carry

    lax.fori_loop(0, count // unroll, body, 0)


def source_kernel(
    w_ref, interp_ref, travel_ref, entry_ref, exit_ref, rows_ref,
    out_ref, table_ref, high_ref, low_ref, wave0, wave1, wave2, rows_scratch,
):
    points = HALF
    zero = jnp.zeros((points, points), jnp.float32)
    for k in range(4):
        for c in range(4):
            block = interp_ref[k, c]
            full = jnp.concatenate(
                [jnp.concatenate([block, zero], 1), jnp.concatenate([zero, block], 1)], 0
            )
            high, low = split(full)
            high_ref[k * LANES : (k + 1) * LANES, c * LANES : (c + 1) * LANES] = high
            low_ref[k * LANES : (k + 1) * LANES, c * LANES : (c + 1) * LANES] = low

    def build(b, carry):
        at = pl.multiple_of(b * LANES, LANES)
        cos_part, sin_part = cos_sin(travel_ref[:, pl.ds(at, LANES)])
        table_ref[pl.ds(at, LANES), :] = jnp.concatenate([cos_part, sin_part], 0).T
        return carry

    lax.fori_loop(0, travel_ref.shape[1] // LANES, build, 0, unroll=2)
    slots = wave0.shape[0]
    gather(table_ref, lambda n: entry_ref[0, n], wave0, slots, 16)
    gather(table_ref, lambda n: exit_ref[0, n], wave1, slots, 16)
    gather(table_ref, lambda n: entry_ref[1, n], wave2, slots, 16)

    count = slots // 4
    lane = lax.broadcasted_iota(jnp.int32, (LANES, LANES), 1)
    rows_scratch[...] = rows_ref[...].astype(jnp.float32).T
    merged = rows_scratch[pl.ds(0, LANES, stride=4), :]
    for a in range(1, 4):
        part = pltpu.roll(rows_scratch[pl.ds(a, LANES, stride=4), :], 32 * a, 1)
        merged = jnp.where(lane >= 32 * a, part, merged)
    out_ref[pl.ds(16, LANES, stride=CHUNK), :] = merged

    for tile in range(count // LANES):
        parts = []
        for c in range(4):
            field = w_ref[pl.ds((c // 2) * 8 + tile * 2 + c % 2, LANES, stride=16), :].T
            wave = wave0[c * count + tile * LANES : c * count + (tile + 1) * LANES, :]
            parts.append(turn(field, wave, -1))
        merged = product(jnp.concatenate(parts, 1), high_ref, low_ref)
        for k in range(4):
            rows = slice(k * count + tile * LANES, k * count + (tile + 1) * LANES)
            field = merged[:, k * LANES : (k + 1) * LANES]
            field = turn(turn(field, wave1[rows, :], 1), wave2[rows, :], -1)
            for n in range(LANES // 4):
                at = (tile * (LANES // 4) + n) * CHUNK + k * 4
                out_ref[at : at + 4, :] = field[4 * n : 4 * n + 4, :]


def target_kernel(
    x_ref, table_ref, high_ref, low_ref,
    out_ref, rows_vmem, rows_smem, wave1, wave2, wave3, middle, last, sem,
):
    rows_vmem[...] = x_ref[pl.ds(16, LANES, stride=CHUNK), :].astype(jnp.int32)
    copy = pltpu.make_async_copy(rows_vmem, rows_smem, sem)
    copy.start()
    copy.wait()

    def body(source, carry):
        for e, wave in enumerate((wave1, wave2, wave3)):
            for k in range(4):
                for a in range(4):
                    row = rows_smem[source, a * 32 + e * 4 + k]
                    wave[pl.ds(source * 16 + k * 4 + a, 1), :] = table_ref[pl.ds(row, 1), :]
        return carry

    lax.fori_loop(0, LANES, body, 0)

    def place(sx, i1, i0, sy, j1, j0):
        return sx * 64 + i1 * 32 + i0 * 16 + sy * 4 + j1 * 2 + j0

    pairs = [(0, 0), (0, 1), (1, 0), (1, 1)]
    for sx in range(2):
        for i1 in range(2):
            outer = [(sy, j1) for sy in range(4) for j1 in range(2)]
            parts = [
                jnp.concatenate(
                    [
                        x_ref[place(sx, i1, i0, sy, j1, j0) * CHUNK : place(sx, i1, i0, sy, j1, j0) * CHUNK + 16, :]
                        for sy, j1 in outer
                    ],
                    0,
                )
                for i0, j0 in pairs
            ]
            merged = product(jnp.concatenate(parts, 1), high_ref, low_ref)
            for q, (i0, j0) in enumerate(pairs):
                for n, (sy, j1) in enumerate(outer):
                    at = place(sx, i1, i0, sy, j1, j0) * 16
                    field = merged[n * 16 : n * 16 + 16, q * LANES : (q + 1) * LANES]
                    field = turn(turn(field, wave1[at : at + 16, :], 1), wave2[at : at + 16, :], -1)
                    middle[at : at + 16, :] = field
    for sx in range(2):
        for i0 in range(2):
            outer = [(sy, j0) for sy in range(4) for j0 in range(2)]
            parts = [
                jnp.concatenate(
                    [
                        middle[place(sx, i1, i0, sy, j1, j0) * 16 : place(sx, i1, i0, sy, j1, j0) * 16 + 16, :]
                        for sy, j0 in outer
                    ],
                    0,
                )
                for i1, j1 in pairs
            ]
            merged = product(jnp.concatenate(parts, 1), high_ref, low_ref)
            for q, (i1, j1) in enumerate(pairs):
                for n, (sy, j0) in enumerate(outer):
                    at = place(sx, i1, i0, sy, j1, j0) * 16
                    field = merged[n * 16 : n * 16 + 16, q * LANES : (q + 1) * LANES]
                    field = turn(field, wave3[at : at + 16, :], 1)
                    group = (sx * 4 + sy) * 16 + i0 * 8 + j0 * 4 + i1 * 2 + j1
                    last[group * CHUNK : group * CHUNK + 16, :] = field
        for sy in range(4):
            base = (sx * 4 + sy) * 16 * CHUNK
            for half in range(2):
                pieces = [
                    last[pl.ds(base + k * 4 + a, 16, stride=CHUNK), :]
                    for a in (2 * half, 2 * half + 1)
                    for k in range(4)
                ]
                out_ref[pl.ds(sx * 8 + half * 4 + sy, LANES, stride=16), :] = jnp.concatenate(pieces, 0).T


def shards(weights, interp, travel, entry_rows, exit_rows):
    count = weights.shape[-1]
    points = interp.shape[-1]
    devices = lax.axis_size("gx") * lax.axis_size("gy")
    slots = 4 * count
    entry = entry_rows.reshape(3, slots)
    exits = exit_rows.reshape(3, slots)
    state = weights.reshape(2 * points, 2, 2, count // LANES, LANES)
    state = state.transpose(0, 1, 3, 2, 4).reshape(slots, LANES)
    rows = jnp.concatenate(
        [exits[1].reshape(4, count), entry[2].reshape(4, count), exits[2].reshape(4, count), jnp.zeros((LANES - 12, count), jnp.int32)]
    )
    f32 = lambda *shape: jax.ShapeDtypeStruct(shape, jnp.float32)
    wave = pltpu.VMEM((slots, LANES), jnp.float32)
    matrix = jax.ShapeDtypeStruct((4 * LANES, 4 * LANES), jnp.bfloat16)
    payload, table, high, low = pl.pallas_call(
        source_kernel,
        out_shape=[f32(devices * CHUNK, LANES), f32(travel.shape[1], LANES), matrix, matrix],
        in_specs=[VMEM, VMEM, VMEM, SMEM, SMEM, VMEM],
        out_specs=[VMEM] * 4,
        scratch_shapes=[wave, wave, wave, pltpu.VMEM((count, LANES), jnp.float32)],
        name="source",
    )(state, interp, travel, entry, exits, rows)
    moved = lax.all_to_all(
        payload.reshape(devices, 1, -1), ("gx", "gy"), split_axis=0, concat_axis=0, tiled=True
    )
    out = pl.pallas_call(
        target_kernel,
        out_shape=f32(slots, LANES),
        in_specs=[VMEM] * 4,
        out_specs=VMEM,
        scratch_shapes=[
            pltpu.VMEM((LANES, LANES), jnp.int32),
            pltpu.SMEM((LANES, LANES), jnp.int32),
            wave,
            wave,
            wave,
            wave,
            pltpu.VMEM((devices * CHUNK, LANES), jnp.float32),
            pltpu.SemaphoreType.DMA,
        ],
        name="target",
    )(moved.reshape(devices * CHUNK, LANES), table, high, low)
    out = out.reshape(2, points, 2, 2, 4, LANES).transpose(0, 1, 2, 4, 3, 5)
    return out.reshape(2, points, 2, 4, 2 * LANES)


def solution(mesh):
    return jax.shard_map(
        shards,
        mesh=mesh,
        in_specs=(
            P(None, None, "gx", "gy", None),
            P(),
            P(),
            P(None, "gx", "gy", None),
            P(None, "gx", "gy", None),
        ),
        out_specs=P(None, None, None, None, ("gx", "gy")),
        check_vma=False,
    )
```

time: 167 us -> 74.7 us (0.45)
  local copies, waits for them, and re-layouts: 94.7 us -> 2.27 us
  Pallas kernels: 0 us -> 40.2 us
  other arithmetic: 33.6 us -> 0.79 us
  matrix products: 6.24 us -> 0 us
    gather x6 -> x0, local copies, waits for them, and re-layouts: 47.7 us -> none  [shards(): look = lambda rows: jnp.take(travel, rows, axis=1)]
    pallas_call x0 -> x2, Pallas kernels: none -> 40.2 us  [the longest x1 24 us: shards(): pl.pallas_call(source_kernel, out_shape=[f32(devices * CHUNK, LANES), f32...]
    sub x3 -> x0, other arithmetic: 11.8 us -> none  [rotate(): cos_part * fields[0] - sin_part * fields[1]]
    reshape x5 -> x0, local copies, waits for them, and re-layouts: 11.4 us -> none  [the longest x1 3.64 us: shards(): fields.reshape(2 * points, 4, devices, own)]
    slice x10 -> x1, local copies, waits for them, and re-layouts: 11.7 us -> 0.78 us  [shards(): exits[1].reshape(4, count)]
    another operation x9 -> x3, local copies, waits for them, and re-layouts: 8.91 us -> 0.03 us  [the longest x1 0.01 us: shards(): exits[1].reshape(4, count)]
    cos x1 -> x0, other arithmetic: 8.26 us -> none  [rotate(): cos_part = jnp.cos(angles)]
    dot_general x3 -> x0, matrix products: 6.24 us -> none  [the longest x1 2.75 us: shards(): jnp.einsum('ijIJts,rsnXaIYbJ->rtnXaiYbj', blocks, fields, precision=high)]
where the time goes in v2:
time: 74.7 us; the launch traced here: 74.4 us
  Pallas kernels  40.2 us (54%)
  blocking collectives  31.1 us (42%)
  local copies, waits for them, and re-layouts  2.27 us (3%)
  other arithmetic  0.79 us (1%)
    all_to_all x1, blocking collectives, shards(): lax.all_to_all(payload.reshape(devices, 1, -1), ('gx', 'gy'), split_axis=...  31.1 us
    pallas_call x1, Pallas kernels, shards(): pl.pallas_call(source_kernel, out_shape=[f32(devices * CHUNK, LANES), f32...  24 us
    pallas_call x1, Pallas kernels, shards(): pl.pallas_call(target_kernel, out_shape=f32(slots, LANES), in_specs=[VMEM...  16.3 us

profile of v2, /device:TPU:1, one launch (start us, length us, event | category | flops | bytes accessed | tf_op | source)
XLA Modules:
  0.0 74.4 jit_solution(2403836278439259176)
XLA Ops:
  0.0 0.8 %slice_reduce_fusion.2 = (s32[2048]{0:T(1024)S(1)}, s32[2048]{0:T(1024)S(1)}, s32[2048]{0:T(1024)S(1)}) fusion(s32[3,1,1,2048]{3,2,1,0:T(1,128)} %param.9, s32[3,1,1,2048]{3,2,1,0:T(1,128)} %param.8), kind=kLoop, calls=%fused_computation.5 | loop fusion | bytes 49152 | tf_op jit(solution)/shard_map/slice | solution.py:211
  0.8 1.4 %copy_bitcast_fusion = (s32[3,2048]{1,0:T(4,128)}, s32[3,2048]{1,0:T(4,128)}) fusion(s32[3,1,1,2048]{3,2,1,0:T(1,128)} %param.9, s32[3,1,1,2048]{3,2,1,0:T(1,128)} %param.8), kind=kLoop, calls=%fused_computation.1 | loop fusion | bytes 98304
  2.2 0.1 pad.3.clone
  2.3 0.8 %add_add_fusion.rows_ref = s32[128,512]{1,0:T(8,128)} fusion(s32[4,512]{1,0:T(4,128)S(1)} %reshape_squeeze.11, s32[4,512]{1,0:T(4,128)S(1)} %reshape_squeeze.10, s32[4,512]{1,0:T(4,128)S(1)} %reshape_squeeze.9, s32[128]{0:T(128)S(1)} %pad.3.clone), kind=kLoop, calls=%fused_computation | loop fusion | flops 196608 | bytes 287232 | tf_op jit(solution)/shard_map/concatenate | solution.py:210
  3.1 24.0 %source.1 = (f32[2176,128]{1,0:T(8,128)}, f32[4096,128]{1,0:T(8,128)}, bf16[512,512]{1,0:T(8,128)(2,1)}, bf16[512,512]{1,0:T(8,128)(2,1)}) custom-call(f32[2048,128]{1,0:T(8,128)} %bitcast.18, f32[4,4,64,64]{3,2,1,0:T(8,128)} %interp_ref.1, f32[64,4096]{1,0:T(8,128)} %travel_ref.1, s32[3,2048]{1,0:T(4,128)} %get-tuple-element.17.entry_ref, ...), custom_call_target="tpu_custom_call" | custom-call | tf_op jit(solution)/shard_map/source/pallas_call | solution.py:216
  27.0 31.1 %all_to_all.5 = f32[128,1,2176]{2,1,0:T(1,128)} all-to-all(f32[128,1,2176]{2,1,0:T(1,128)} %bitcast.17), channel_id=1, replica_groups=mesh['gx'=8,'gy'=16] {'gx','gy'}, dimensions={0} | all-to-all | bytes 2228224 | tf_op jit(solution)/shard_map/all_to_all | solution.py:224
  58.1 16.3 %target.1 = f32[2048,128]{1,0:T(8,128)} custom-call(f32[2176,128]{1,0:T(8,128)} %bitcast.16, f32[4096,128]{1,0:T(8,128)} %get-tuple-element.10.table_ref, bf16[512,512]{1,0:T(8,128)(2,1)} %get-tuple-element.11.high_ref, bf16[512,512]{1,0:T(8,128)(2,1)} %get-tuple-element.12.low_ref), custom_call_target="tpu_custom_call" | custom-call | tf_op jit(solution)/shard_map/target/pallas_call | solution.py:227
  (4 shorter events, 0.0 us)

commit v3 on v1

v3 whole, which is shorter than its diff:
```python
import jax
import jax.numpy as jnp
from jax import lax
from jax.experimental import pallas as pl
from jax.experimental.pallas import tpu as pltpu
from jax.sharding import PartitionSpec as P

LANES = 128
HALF = 64
CHUNK = 17
WIDE = 256
VMEM = pl.BlockSpec(memory_space=pltpu.VMEM)
HBM = pl.BlockSpec(memory_space=pltpu.HBM)
PIECES = 4


def cos_sin(x):
    z = x * x
    s = SIN[-1]
    for term in SIN[-2::-1]:
        s = s * z + term
    s = s * x
    c = COS[-1]
    for term in COS[-2::-1]:
        c = c * z + term
    return 1.0 - s * s, s * c


SIN = (0.70710677, -0.029462768, 3.682721e-4, -2.1885735e-6, 7.1936523e-9)
COS = (1.4142135, -0.17677669, 3.682845e-3, -3.0689214e-5, 1.3677929e-7, -3.5967443e-10)


def swap(x):
    return pltpu.roll(x, HALF, 1)


def low_half(x):
    return lax.broadcasted_iota(jnp.int32, x.shape, 1) < HALF


def interleave(first, second):
    low = low_half(first)
    return jnp.where(low, first, swap(second)), jnp.where(low, swap(first), second)


def modulate(wave, real, imag):
    cos_part, sin_part = wave
    return cos_part * real - sin_part * imag, sin_part * real + cos_part * imag


def demodulate(wave, real, imag):
    cos_part, sin_part = wave
    return cos_part * real + sin_part * imag, cos_part * imag - sin_part * real


def split(x):
    high = x.astype(jnp.bfloat16)
    low = (x - high.astype(jnp.float32)).astype(jnp.bfloat16)
    return high, low


def put(ref, row, block, x):
    high, low = split(x)
    for part, value in enumerate((high, low, high)):
        at = part * WIDE + block * LANES
        ref[pl.ds(row, x.shape[0]), at : at + LANES] = value


def dot(x_ref, matrix_ref, out_ref):
    out_ref[...] = jnp.dot(x_ref[...], matrix_ref[...], preferred_element_type=jnp.float32)


def source_kernel(
    w_hbm, interp_hbm, travel_hbm, entry_hbm, exit_hbm,
    out_ref, table_ref, matrix_ref,
    w_ref, interp_ref, travel_ref, entry_vmem, exit_vmem, entry_ref, exit_ref,
    wave0, wave1, wave2, rows_scratch, x_ref, merged, sems,
):
    width = travel_ref.shape[1] // PIECES
    piece = lambda p: (slice(None), slice(p * width, (p + 1) * width))
    copies = [
        pltpu.make_async_copy(travel_hbm.at[piece(p)], travel_ref.at[piece(p)], sems.at[p])
        for p in range(PIECES)
    ]
    operands = (
        (entry_hbm.at[:32], entry_ref),
        (exit_hbm.at[:16], exit_ref),
        (w_hbm, w_ref),
        (interp_hbm, interp_ref),
        (entry_hbm, entry_vmem),
        (exit_hbm, exit_vmem),
    )
    copies += [
        pltpu.make_async_copy(*pair, sems.at[PIECES + n]) for n, pair in enumerate(operands)
    ]
    for copy in copies:
        copy.start()

    def build(b, carry):
        at = pl.multiple_of(b * LANES, LANES)
        cos_part, sin_part = cos_sin(travel_ref[:, pl.ds(at, LANES)])
        table_ref[pl.ds(at, LANES), :] = jnp.concatenate([cos_part, sin_part], 0).T
        return carry

    blocks = width // LANES
    for p in range(PIECES):
        copies[p].wait()
        lax.fori_loop(p * blocks, (p + 1) * blocks, build, 0, unroll=4)
    for copy in copies[PIECES : PIECES + 2]:
        copy.wait()

    def gather(step, carry):
        at = step * LANES
        for n in range(LANES):
            wave0[pl.ds(at + n, 1), :] = table_ref[pl.ds(entry_ref[step, n], 1), :]
            wave1[pl.ds(at + n, 1), :] = table_ref[pl.ds(exit_ref[step, n], 1), :]
            wave2[pl.ds(at + n, 1), :] = table_ref[pl.ds(entry_ref[step + 16, n], 1), :]
        return carry

    lax.fori_loop(0, wave0.shape[0] // LANES, gather, 0)
    for copy in copies[PIECES + 2 :]:
        copy.wait()

    for kp in range(2):
        for cp in range(2):
            rows = [
                jnp.concatenate([interp_ref[2 * kp + kk, 2 * cp], interp_ref[2 * kp + kk, 2 * cp + 1]], 1)
                for kk in range(2)
            ]
            high, low = split(jnp.concatenate(rows, 0).T)
            for part, value in enumerate((high, high, low)):
                at = part * WIDE + cp * LANES
                matrix_ref[at : at + LANES, kp * LANES : (kp + 1) * LANES] = value

    tiles = rows_scratch.shape[0] // LANES
    zero = jnp.zeros((LANES - 12, LANES), jnp.float32)
    for tile in range(tiles):
        rows = [
            exit_vmem[pl.ds(16 + tile, 8, stride=tiles), :].astype(jnp.float32),
            entry_vmem[pl.ds(32 + tile, 4, stride=tiles), :].astype(jnp.float32),
            zero,
        ]
        rows_scratch[tile * LANES : (tile + 1) * LANES, :] = jnp.concatenate(rows, 0).T
    lane = lax.broadcasted_iota(jnp.int32, (LANES, LANES), 1)
    indices = rows_scratch[pl.ds(0, LANES, stride=4), :]
    for a in range(1, 4):
        part = pltpu.roll(rows_scratch[pl.ds(a, LANES, stride=4), :], 16 * a, 1)
        indices = jnp.where(lane >= 16 * a, part, indices)
    out_ref[pl.ds(16, LANES, stride=CHUNK), :] = indices

    count = tiles * LANES

    def pair(wave, p, at):
        return interleave(
            *[wave[pl.ds(pl.multiple_of(n * count + at, LANES), LANES), :] for n in (2 * p, 2 * p + 1)]
        )

    def enter(tile, carry):
        at = pl.multiple_of(tile * LANES, LANES)
        for cx in range(2):
            parts = []
            for r in range(2):
                start = r * HALF * 16 + cx * 8 + tile * 2
                block = [w_ref[pl.ds(start + cy, HALF, stride=16), :] for cy in range(2)]
                parts.append(jnp.concatenate(block, 0).T)
            real, imag = demodulate(pair(wave0, cx, at), *parts)
            put(x_ref, at, cx, real)
            put(x_ref, pl.multiple_of(count + at, LANES), cx, imag)
        return carry

    lax.fori_loop(0, tiles, enter, 0)
    dot(x_ref, matrix_ref, merged)

    def leave(tile, carry):
        at = pl.multiple_of(tile * LANES, LANES)
        sent = out_ref.at[pl.ds(pl.multiple_of(tile * (LANES // 4) * CHUNK, 8), (LANES // 4) * CHUNK), :]
        for kp in range(2):
            block = slice(kp * LANES, (kp + 1) * LANES)
            real = merged[pl.ds(at, LANES), block]
            imag = merged[pl.ds(pl.multiple_of(count + at, LANES), LANES), block]
            fields = modulate(pair(wave1, kp, at), real, imag)
            fields = demodulate(pair(wave2, kp, at), *fields)
            for r in range(2):
                for n in range(LANES // 4):
                    to = n * CHUNK + r * 8 + kp * 4
                    sent[to : to + 4, :] = fields[r][4 * n : 4 * n + 4, :]
        return carry

    lax.fori_loop(0, tiles, leave, 0)


def target_kernel(
    x_ref, table_ref, matrix_ref,
    out_ref, rows_vmem, rows_smem, wave1, wave2, wave3, x1_ref, x2_ref, merged, last, sems,
):
    count = rows_vmem.shape[0]
    indices = [x_ref[pl.ds(16 + n * CHUNK, count, stride=2 * CHUNK), :] for n in range(2)]
    rows_vmem[...] = jnp.where(low_half(indices[0]), indices[0], swap(indices[1])).astype(jnp.int32)
    size = count // PIECES
    copies = []
    for p in range(PIECES):
        part = slice(p * size, (p + 1) * size)
        copies.append(pltpu.make_async_copy(rows_vmem.at[part], rows_smem.at[part], sems.at[p]))
        copies[-1].start()

    bits = range(2)

    def first(step, carry):
        base = 32 * CHUNK
        part = x_ref.at[pl.ds(pl.multiple_of(step * base, 8), base), :]
        for sy in range(4):
            for j1 in bits:
                group = pl.multiple_of(step * 256 + (sy * 2 + j1) * 32, 32)
                for i0 in bits:
                    at = [(i0 * 16 + sy * 4 + j1 * 2 + j0) * CHUNK for j0 in bits]
                    parts = interleave(*[part[a : a + 16, :] for a in at])
                    rows = [parts[kk][8 * r : 8 * r + 8] for r in bits for kk in bits]
                    put(x1_ref, group, i0, jnp.concatenate(rows, 0))
        return carry

    lax.fori_loop(0, 4, first, 0)
    dot(x1_ref, matrix_ref, merged)

    def gather(row, carry):
        for n in range(2):
            for e, wave in enumerate((wave1, wave3, wave2)):
                for k in range(4):
                    for a in range(4):
                        index = rows_smem[row, n * HALF + a * 16 + e * 4 + k]
                        at = row * 32 + n * 16 + (k % 2) * 8 + (k // 2) * 4 + a
                        wave[pl.ds(at, 1), :] = table_ref[pl.ds(index, 1), :]
        return carry

    for p in range(PIECES):
        copies[p].wait()
        lax.fori_loop(p * size, (p + 1) * size, gather, 0)

    def rows_of(ref, base, offset, block=slice(None), size=16):
        return ref[pl.ds(pl.multiple_of(base + offset, 16), size), block]

    def second(n, carry):
        sx, sy = n // 4, n % 4
        ends = (sx * 64 + sy * 4) * 16
        for i1 in bits:
            for i0 in bits:
                fields = []
                for j1 in bits:
                    group = sx * 512 + sy * 64
                    offset = i1 * 256 + j1 * 32
                    block = slice(i0 * LANES, (i0 + 1) * LANES)
                    field = [rows_of(merged, group, offset + r * 16, block) for r in bits]
                    pair = [
                        interleave(
                            *[rows_of(wave, ends, (i1 * 32 + i0 * 16 + j1 * 2 + j0) * 16) for j0 in bits]
                        )
                        for wave in (wave1, wave2)
                    ]
                    field = modulate(pair[0], *field)
                    fields.append(demodulate(pair[1], *field))
                for r in bits:
                    parts = interleave(fields[0][r], fields[1][r])
                    for j0 in bits:
                        put(x2_ref, pl.multiple_of(n * 128 + (i0 * 2 + j0) * 32 + r * 16, 16), i1, parts[j0])
        return carry

    lax.fori_loop(0, 8, second, 0)
    dot(x2_ref, matrix_ref, merged)

    def third(n, carry):
        sx, sy = n // 4, n % 4
        ends = (sx * 64 + sy * 4) * 16
        for i0 in bits:
            for j0 in bits:
                for i1 in bits:
                    block = slice(i1 * LANES, (i1 + 1) * LANES)
                    field = [
                        rows_of(merged, n * 128, (i0 * 2 + j0) * 32 + r * 16, block) for r in bits
                    ]
                    pair = interleave(
                        *[rows_of(wave3, ends, (i1 * 32 + i0 * 16 + j1 * 2 + j0) * 16) for j1 in bits]
                    )
                    field = interleave(*modulate(pair, *field))
                    for j1 in bits:
                        at = (i0 * 8 + j0 * 4 + i1 * 2 + j1) * CHUNK
                        last[at : at + 16, :] = field[j1]
        for half in bits:
            pieces = [
                last[pl.ds((k % 2) * 8 + (k // 2) * 4 + a, 16, stride=CHUNK), :]
                for a in (2 * half, 2 * half + 1)
                for k in range(4)
            ]
            out_ref[pl.ds(sx * 8 + half * 4 + sy, LANES, stride=16), :] = jnp.concatenate(pieces, 0).T
        return carry

    lax.fori_loop(0, 8, third, 0)


def shards(weights, interp, travel, entry_rows, exit_rows):
    count = weights.shape[-1]
    points = interp.shape[-1]
    devices = lax.axis_size("gx") * lax.axis_size("gy")
    slots = 4 * count
    entry = entry_rows.reshape(3 * slots // LANES, LANES)
    exits = exit_rows.reshape(3 * slots // LANES, LANES)
    state = weights.reshape(2 * points, 2, 2, count // LANES, LANES)
    state = state.transpose(0, 1, 3, 2, 4).reshape(slots, LANES)
    f32 = lambda *shape: jax.ShapeDtypeStruct(shape, jnp.float32)
    vmem = lambda *shape: pltpu.VMEM(shape, jnp.float32)
    left = pltpu.VMEM((slots // 2, 3 * WIDE), jnp.bfloat16)
    params = pltpu.CompilerParams(vmem_limit_bytes=28 << 20)
    payload, table, matrix = pl.pallas_call(
        source_kernel,
        out_shape=[
            f32(devices * CHUNK, LANES),
            f32(travel.shape[1], LANES),
            jax.ShapeDtypeStruct((3 * WIDE, WIDE), jnp.bfloat16),
        ],
        in_specs=[HBM] * 5,
        out_specs=[VMEM] * 3,
        scratch_shapes=[
            vmem(slots, LANES),
            vmem(*interp.shape),
            vmem(*travel.shape),
            pltpu.VMEM(entry.shape, jnp.int32),
            pltpu.VMEM(exits.shape, jnp.int32),
            pltpu.SMEM((32, LANES), jnp.int32),
            pltpu.SMEM((16, LANES), jnp.int32),
            vmem(slots, LANES),
            vmem(slots, LANES),
            vmem(slots, LANES),
            vmem(count, LANES),
            left,
            vmem(slots // 2, WIDE),
            pltpu.SemaphoreType.DMA((PIECES + 6,)),
        ],
        compiler_params=params,
        name="source",
    )(*[pltpu.with_memory_space_constraint(x, pltpu.HBM) for x in (state, interp, travel, entry, exits)])
    moved = lax.all_to_all(
        payload.reshape(devices, 1, -1), ("gx", "gy"), split_axis=0, concat_axis=0, tiled=True
    )
    out = pl.pallas_call(
        target_kernel,
        out_shape=f32(slots, LANES),
        in_specs=[VMEM] * 3,
        out_specs=VMEM,
        scratch_shapes=[
            pltpu.VMEM((HALF, LANES), jnp.int32),
            pltpu.SMEM((HALF, LANES), jnp.int32),
            vmem(slots, LANES),
            vmem(slots, LANES),
            vmem(slots, LANES),
            left,
            left,
            vmem(slots // 2, WIDE),
            vmem(16 * CHUNK, LANES),
            pltpu.SemaphoreType.DMA((PIECES,)),
        ],
        compiler_params=params,
        name="target",
    )(moved.reshape(devices * CHUNK, LANES), table, matrix)
    out = out.reshape(2, points, 2, 2, 4, LANES).transpose(0, 1, 2, 4, 3, 5)
    return out.reshape(2, points, 2, 4, 2 * LANES)


def solution(mesh):
    return jax.shard_map(
        shards,
        mesh=mesh,
        in_specs=(
            P(None, None, "gx", "gy", None),
            P(),
            P(),
            P(None, "gx", "gy", None),
            P(None, "gx", "gy", None),
        ),
        out_specs=P(None, None, None, None, ("gx", "gy")),
        check_vma=False,
    )
```

time: 167 us -> 53.6 us (0.32)
  local copies, waits for them, and re-layouts: 94.7 us -> 0 us
  other arithmetic: 33.6 us -> 0 us
  Pallas kernels: 0 us -> 22.6 us
  matrix products: 6.24 us -> 0 us
    gather x6 -> x0, local copies, waits for them, and re-layouts: 47.7 us -> none  [shards(): look = lambda rows: jnp.take(travel, rows, axis=1)]
    pallas_call x0 -> x2, Pallas kernels: none -> 22.6 us  [the longest x1 12.8 us: shards(): pl.pallas_call(target_kernel, out_shape=f32(slots, LANES), in_specs=[VMEM...]
    sub x3 -> x0, other arithmetic: 11.8 us -> none  [rotate(): cos_part * fields[0] - sin_part * fields[1]]
    slice x10 -> x0, local copies, waits for them, and re-layouts: 11.7 us -> none  [the longest x5 5.42 us: rotate(): fields[0]]
    reshape x5 -> x0, local copies, waits for them, and re-layouts: 11.4 us -> none  [the longest x1 3.64 us: shards(): fields.reshape(2 * points, 4, devices, own)]
    another operation x9 -> x0, local copies, waits for them, and re-layouts: 8.91 us -> none  [the longest x3 7.79 us: rotate(): jnp.stack([cos_part * fields[0] - sin_part * fields[1], sin_part * fields...]
    cos x1 -> x0, other arithmetic: 8.26 us -> none  [rotate(): cos_part = jnp.cos(angles)]
    dot_general x3 -> x0, matrix products: 6.24 us -> none  [the longest x1 2.75 us: shards(): jnp.einsum('ijIJts,rsnXaIYbJ->rtnXaiYbj', blocks, fields, precision=high)]
where the time goes in v3:
time: 53.6 us; the launch traced here: 53.4 us
  blocking collectives  30.8 us (57%)
  Pallas kernels  22.6 us (42%)
    all_to_all x1, blocking collectives, shards(): lax.all_to_all(payload.reshape(devices, 1, -1), ('gx', 'gy'), split_axis=...  30.8 us
    pallas_call x1, Pallas kernels, shards(): pl.pallas_call(target_kernel, out_shape=f32(slots, LANES), in_specs=[VMEM...  12.8 us
    pallas_call x1, Pallas kernels, shards(): pl.pallas_call(source_kernel, out_shape=[f32(devices * CHUNK, LANES), f32...  9.8 us

profile of v3, /device:TPU:1, one launch (start us, length us, event | category | flops | bytes accessed | tf_op | source)
XLA Modules:
  0.0 53.4 jit_solution(8649896505202298458)
XLA Ops:
  0.0 9.8 %source.1 = (f32[2176,128]{1,0:T(8,128)S(1)}, f32[4096,128]{1,0:T(8,128)S(1)}, bf16[768,256]{1,0:T(8,128)(2,1)S(1)}) custom-call(f32[2048,128]{1,0:T(8,128)} %bitcast.16, f32[4,4,64,64]{3,2,1,0:T(8,128)} %interp_hbm.1, f32[64,4096]{1,0:T(8,128)} %travel_hbm.1, s32[48,128]{1,0:T(8,128)} %bitcast.17, s32[48,128]{1,0:T(8,128)} %bitcast.18), custom_call_target="tpu_custom_call" | custom-call | tf_op jit(solution)/shard_map/source/pallas_call | solution.py:311
  9.8 30.8 %all_to_all.5 = f32[128,1,2176]{2,1,0:T(1,128)S(1)} all-to-all(f32[128,1,2176]{2,1,0:T(1,128)S(1)} %bitcast.15), channel_id=1, replica_groups=mesh['gx'=8,'gy'=16] {'gx','gy'}, dimensions={0} | all-to-all | bytes 2228224 | tf_op jit(solution)/shard_map/all_to_all | solution.py:339
  40.6 12.8 %target.1 = f32[2048,128]{1,0:T(8,128)} custom-call(f32[2176,128]{1,0:T(8,128)S(1)} %bitcast.14, f32[4096,128]{1,0:T(8,128)S(1)} %get-tuple-element.9.table_ref, bf16[768,256]{1,0:T(8,128)(2,1)S(1)} %get-tuple-element.10.matrix_ref), custom_call_target="tpu_custom_call" | custom-call | tf_op jit(solution)/shard_map/target/pallas_call | solution.py:342

commit v4 on v3

v4 whole, which is shorter than its diff:
```python
import jax
import jax.numpy as jnp
from jax import lax
from jax.experimental import pallas as pl
from jax.experimental.pallas import tpu as pltpu
from jax.sharding import PartitionSpec as P

LANES = 128
HALF = 64
CHUNK = 17
WIDE = 256
VMEM = pl.BlockSpec(memory_space=pltpu.VMEM)
HBM = pl.BlockSpec(memory_space=pltpu.HBM)
PIECES = 4


def cos_sin(x):
    z = x * x
    s = SIN[-1]
    for term in SIN[-2::-1]:
        s = s * z + term
    s = s * x
    c = COS[-1]
    for term in COS[-2::-1]:
        c = c * z + term
    return 1.0 - s * s, s * c


SIN = (0.70710677, -0.029462768, 3.682721e-4, -2.1885735e-6, 7.1936523e-9)
COS = (1.4142135, -0.17677669, 3.682845e-3, -3.0689214e-5, 1.3677929e-7, -3.5967443e-10)


def swap(x):
    return pltpu.roll(x, HALF, 1)


def low_half(x):
    return lax.broadcasted_iota(jnp.int32, x.shape, 1) < HALF


def interleave(first, second):
    low = low_half(first)
    moved = swap(jnp.where(low, second, first))
    return jnp.where(low, first, moved), jnp.where(low, moved, second)


def modulate(wave, real, imag):
    cos_part, sin_part = wave
    return cos_part * real - sin_part * imag, sin_part * real + cos_part * imag


def demodulate(wave, real, imag):
    cos_part, sin_part = wave
    return cos_part * real + sin_part * imag, cos_part * imag - sin_part * real


def split(x):
    high = x.astype(jnp.bfloat16)
    low = (x - high.astype(jnp.float32)).astype(jnp.bfloat16)
    return high, low


def put(ref, row, block, x):
    high, low = split(x)
    for part, value in enumerate((high, low, high)):
        at = part * WIDE + block * LANES
        ref[pl.ds(row, x.shape[0]), at : at + LANES] = value


def dot(x_ref, matrix_ref, between=lambda: None):
    total = None
    for part in range(3):
        at = slice(part * WIDE, (part + 1) * WIDE)
        term = jnp.dot(x_ref[:, at], matrix_ref[at, :], preferred_element_type=jnp.float32)
        total = term if total is None else total + term
        between()
    return total


def source_kernel(
    w_hbm, interp_hbm, travel_hbm, entry_hbm, exit_hbm, entry_rows_hbm, exit_rows_hbm,
    out_ref, table_ref, matrix_ref,
    w_ref, interp_ref, travel_ref, entry_vmem, exit_vmem, entry_ref, exit_ref, next_ref,
    wave0, wave1, wave2, rows_scratch, x_ref, merged, sems,
):
    slots = wave0.shape[0]
    width = travel_ref.shape[1] // PIECES

    def piece(p):
        at = (slice(None), pl.ds(pl.multiple_of(p * width, width), width))
        return pltpu.make_async_copy(travel_hbm.at[at], travel_ref.at[at], sems.at[p])

    operands = (
        (interp_hbm, interp_ref),
        (entry_rows_hbm, entry_vmem),
        (exit_rows_hbm, exit_vmem),
        (entry_hbm.at[:slots], entry_ref),
        (exit_hbm.at[:slots], exit_ref),
        (entry_hbm.at[slots : 2 * slots], next_ref),
        (w_hbm, w_ref),
    )
    copies = [
        pltpu.make_async_copy(*pair, sems.at[PIECES + n]) for n, pair in enumerate(operands)
    ]
    for copy in copies[:3]:
        copy.start()
    for p in range(PIECES):
        piece(p).start()
    for copy in copies[3:]:
        copy.start()

    for copy in copies[:3]:
        copy.wait()
    for kp in range(2):
        for cp in range(2):
            rows = [
                jnp.concatenate([interp_ref[2 * kp + kk, 2 * cp], interp_ref[2 * kp + kk, 2 * cp + 1]], 1)
                for kk in range(2)
            ]
            high, low = split(jnp.concatenate(rows, 0).T)
            for part, value in enumerate((high, high, low)):
                at = part * WIDE + cp * LANES
                matrix_ref[at : at + LANES, kp * LANES : (kp + 1) * LANES] = value

    tiles = rows_scratch.shape[0] // LANES
    for tile in range(tiles):
        rows = []
        for ref, e in ((exit_vmem, 1), (entry_vmem, 2), (exit_vmem, 2)):
            rows.append(ref[pl.ds(16 * e + tile, 4, stride=tiles), :].astype(jnp.float32))
            rows.append(jnp.zeros((12, LANES), jnp.float32))
        rows.append(jnp.zeros((LANES - 48, LANES), jnp.float32))
        rows_scratch[tile * LANES : (tile + 1) * LANES, :] = jnp.concatenate(rows, 0).T
    lane = lax.broadcasted_iota(jnp.int32, (LANES, LANES), 1)
    indices = rows_scratch[pl.ds(0, LANES, stride=4), :]
    for a in range(1, 4):
        part = pltpu.roll(rows_scratch[pl.ds(a, LANES, stride=4), :], 4 * a, 1)
        indices = jnp.where((lane & 15) >= 4 * a, part, indices)
    out_ref[pl.ds(16, LANES, stride=CHUNK), :] = indices

    def build(p, carry):
        piece(p).wait()

        def block(b, carry):
            at = pl.multiple_of(p * width + b * 2 * LANES, 2 * LANES)
            cos_part, sin_part = cos_sin(travel_ref[:, pl.ds(at, 2 * LANES)])
            table_ref[pl.ds(at, 2 * LANES), :] = jnp.concatenate([cos_part, sin_part], 0).T
            return carry

        return lax.fori_loop(0, width // (2 * LANES), block, carry)

    lax.fori_loop(0, PIECES, build, 0)
    for copy in copies[3:]:
        copy.wait()

    size = 64

    def gather(step, carry):
        at = step * size
        for n in range(size):
            wave0[pl.ds(at + n, 1), :] = table_ref[pl.ds(entry_ref[at + n], 1), :]
        return carry

    lax.fori_loop(0, slots // size, gather, 0)

    count = tiles * LANES

    def pair(wave, p, at):
        return interleave(
            *[wave[pl.ds(pl.multiple_of(n * count + at, LANES), LANES), :] for n in (2 * p, 2 * p + 1)]
        )

    def enter(tile, carry):
        at = pl.multiple_of(tile * LANES, LANES)
        chunks = iter(range(8))

        def between():
            base = tile * 4 * LANES + next(chunks) * HALF
            for n in range(HALF):
                wave1[pl.ds(base + n, 1), :] = table_ref[pl.ds(exit_ref[base + n], 1), :]
                wave2[pl.ds(base + n, 1), :] = table_ref[pl.ds(next_ref[base + n], 1), :]

        for cx in range(2):
            parts = []
            for r in range(2):
                start = r * HALF * 16 + cx * 8 + tile * 2
                block = [w_ref[pl.ds(start + cy, HALF, stride=16), :] for cy in range(2)]
                parts.append(jnp.concatenate(block, 0).T)
            between()
            real, imag = demodulate(pair(wave0, cx, at), *parts)
            put(x_ref, 0, cx, real)
            put(x_ref, LANES, cx, imag)
            between()
        between()
        merged[pl.ds(pl.multiple_of(tile * WIDE, WIDE), WIDE), :] = dot(x_ref, matrix_ref, between)
        return carry

    lax.fori_loop(0, tiles, enter, 0)

    def leave(tile, carry):
        at = pl.multiple_of(tile * LANES, LANES)
        sent = out_ref.at[pl.ds(pl.multiple_of(tile * (LANES // 4) * CHUNK, 8), (LANES // 4) * CHUNK), :]
        for kp in range(2):
            block = slice(kp * LANES, (kp + 1) * LANES)
            real, imag = [
                merged[pl.ds(pl.multiple_of(tile * WIDE + r * LANES, LANES), LANES), block] for r in range(2)
            ]
            fields = modulate(pair(wave1, kp, at), real, imag)
            fields = demodulate(pair(wave2, kp, at), *fields)
            for r in range(2):
                for n in range(LANES // 4):
                    to = n * CHUNK + r * 8 + kp * 4
                    sent[to : to + 4, :] = fields[r][4 * n : 4 * n + 4, :]
        return carry

    lax.fori_loop(0, tiles, leave, 0)


def target_kernel(
    x_ref, table_ref, matrix_ref,
    out_ref, rows_vmem, waves, more_waves, x1_ref, x2_ref, merged, result, last, sems, *rows_smem,
):
    rows_vmem[...] = x_ref[pl.ds(16, LANES, stride=CHUNK), :].astype(jnp.int32).T
    copies = [
        pltpu.make_async_copy(rows_vmem.at[pl.ds(n, 1), :], to, sems.at[n]) for n, to in enumerate(rows_smem)
    ]
    for copy in copies:
        copy.start()

    bits = range(2)

    def first(step, carry):
        base = 32 * CHUNK
        part = x_ref.at[pl.ds(pl.multiple_of(step * base, 8), base), :]
        for sy in range(4):
            for j1 in bits:
                group = pl.multiple_of(step * 256 + (sy * 2 + j1) * 32, 32)
                for i0 in bits:
                    at = [(i0 * 16 + sy * 4 + j1 * 2 + j0) * CHUNK for j0 in bits]
                    parts = interleave(*[part[a : a + 16, :] for a in at])
                    rows = [parts[kk][8 * r : 8 * r + 8] for r in bits for kk in bits]
                    put(x1_ref, group, i0, jnp.concatenate(rows, 0))
        return carry

    lax.fori_loop(0, 4, first, 0)

    merged[:512, :] = dot(x1_ref.at[:512, :], matrix_ref)
    for copy in copies:
        copy.wait()

    def gather(n, wave):
        base = n // 4 * 64 + n % 4 * 4
        chunks = iter(range(16))

        def chunk():
            b = next(chunks)
            source = base + (b >> 2) * 16 + b % 4
            for e in range(3):
                for k in range(4):
                    for a in range(4):
                        index = rows_smem[e * 16 + a * 4 + k][0, source]
                        at = e * 256 + b * 16 + k % 2 * 8 + k // 2 * 4 + a
                        wave[at : at + 1, :] = table_ref[pl.ds(index, 1), :]

        return chunk

    def levels(n, wave, between):
        sx, sy = n // 4, n % 4

        def pair(to, ends):
            at = [to * 256 + ((i1 * 2 + i0) * 4 + j1 * 2 + j0) * 16 for i1, i0, j1, j0 in ends]
            return interleave(*[wave[a : a + 16, :] for a in at])

        for i1 in bits:
            for i0 in bits:
                fields = []
                block = slice(i0 * LANES, (i0 + 1) * LANES)
                for j1 in bits:
                    group = sx * 512 + sy * 64 + i1 * 256 + j1 * 32
                    field = [
                        merged[pl.ds(pl.multiple_of(group + r * 16, 16), 16), block] for r in bits
                    ]
                    ends = [(i1, i0, j1, j0) for j0 in bits]
                    field = modulate(pair(0, ends), *field)
                    fields.append(demodulate(pair(1, ends), *field))
                for r in bits:
                    parts = interleave(fields[0][r], fields[1][r])
                    for j0 in bits:
                        put(x2_ref, (i0 * 2 + j0) * 32 + r * 16, i1, parts[j0])
                    between()
        result[...] = dot(x2_ref, matrix_ref, between)
        for i0 in bits:
            for j0 in bits:
                for i1 in bits:
                    block = slice(i1 * LANES, (i1 + 1) * LANES)
                    group = (i0 * 2 + j0) * 32
                    field = [result[group + r * 16 : group + r * 16 + 16, block] for r in bits]
                    field = interleave(*modulate(pair(2, [(i1, i0, j1, j0) for j1 in bits]), *field))
                    for j1 in bits:
                        at = (i0 * 8 + j0 * 4 + i1 * 2 + j1) * CHUNK
                        last[at : at + 16, :] = field[j1]
                between()
        for half in bits:
            pieces = [
                last[pl.ds((k % 2) * 8 + (k // 2) * 4 + a, 16, stride=CHUNK), :]
                for a in (2 * half, 2 * half + 1)
                for k in range(4)
            ]
            out_ref[pl.ds(sx * 8 + half * 4 + sy, LANES, stride=16), :] = jnp.concatenate(pieces, 0).T
            if half == 0:
                between()

    chunk = gather(0, waves)

    def some():
        for _ in range(5):
            chunk()

    merged[512:, :] = dot(x1_ref.at[512:, :], matrix_ref, some)
    chunk()

    def two(m, carry):
        levels(2 * m, waves, gather(2 * m + 1, more_waves))
        levels(2 * m + 1, more_waves, gather((2 * m + 2) % 8, waves))
        return carry

    lax.fori_loop(0, 4, two, 0)


def shards(weights, interp, travel, entry_rows, exit_rows):
    count = weights.shape[-1]
    points = interp.shape[-1]
    devices = lax.axis_size("gx") * lax.axis_size("gy")
    slots = 4 * count
    entry = entry_rows.reshape(3 * slots // LANES, LANES)
    exits = exit_rows.reshape(3 * slots // LANES, LANES)
    state = weights.reshape(2 * points, 2, 2, count // LANES, LANES)
    state = state.transpose(0, 1, 3, 2, 4).reshape(slots, LANES)
    f32 = lambda *shape: jax.ShapeDtypeStruct(shape, jnp.float32)
    vmem = lambda *shape: pltpu.VMEM(shape, jnp.float32)
    params = pltpu.CompilerParams(vmem_limit_bytes=28 << 20)
    operands = state, interp, travel, entry_rows.reshape(-1), exit_rows.reshape(-1), entry, exits
    payload, table, matrix = pl.pallas_call(
        source_kernel,
        out_shape=[
            f32(devices * CHUNK, LANES),
            f32(travel.shape[1], LANES),
            jax.ShapeDtypeStruct((3 * WIDE, WIDE), jnp.bfloat16),
        ],
        in_specs=[HBM] * 7,
        out_specs=[VMEM] * 3,
        scratch_shapes=[
            vmem(slots, LANES),
            vmem(*interp.shape),
            vmem(*travel.shape),
            pltpu.VMEM(entry.shape, jnp.int32),
            pltpu.VMEM(exits.shape, jnp.int32),
            pltpu.SMEM((slots,), jnp.int32),
            pltpu.SMEM((slots,), jnp.int32),
            pltpu.SMEM((slots,), jnp.int32),
            vmem(slots, LANES),
            vmem(slots, LANES),
            vmem(slots, LANES),
            vmem(count, LANES),
            pltpu.VMEM((WIDE, 3 * WIDE), jnp.bfloat16),
            vmem(slots // 2, WIDE),
            pltpu.SemaphoreType.DMA((PIECES + 7,)),
        ],
        compiler_params=params,
        name="source",
    )(*[pltpu.with_memory_space_constraint(x, pltpu.HBM) for x in operands])
    moved = lax.all_to_all(
        payload.reshape(devices, 1, -1), ("gx", "gy"), split_axis=0, concat_axis=0, tiled=True
    )
    out = pl.pallas_call(
        target_kernel,
        out_shape=f32(slots, LANES),
        in_specs=[VMEM] * 3,
        out_specs=VMEM,
        scratch_shapes=[
            pltpu.VMEM((LANES, LANES), jnp.int32),
            vmem(3 * 256, LANES),
            vmem(3 * 256, LANES),
            pltpu.VMEM((slots // 2, 3 * WIDE), jnp.bfloat16),
            pltpu.VMEM((LANES, 3 * WIDE), jnp.bfloat16),
            vmem(slots // 2, WIDE),
            vmem(LANES, WIDE),
            vmem(16 * CHUNK, LANES),
            pltpu.SemaphoreType.DMA((48,)),
        ]
        + [pltpu.SMEM((1, LANES), jnp.int32)] * 48,
        compiler_params=params,
        name="target",
    )(moved.reshape(devices * CHUNK, LANES), table, matrix)
    out = out.reshape(2, points, 2, 2, 4, LANES).transpose(0, 1, 2, 4, 3, 5)
    return out.reshape(2, points, 2, 4, 2 * LANES)


def solution(mesh):
    return jax.shard_map(
        shards,
        mesh=mesh,
        in_specs=(
            P(None, None, "gx", "gy", None),
            P(),
            P(),
            P(None, "gx", "gy", None),
            P(None, "gx", "gy", None),
        ),
        out_specs=P(None, None, None, None, ("gx", "gy")),
        check_vma=False,
    )
```

time: 53.6 us -> 50 us (0.933)
  Pallas kernels: 22.6 us -> 19 us
    pallas_call x1, Pallas kernels: 12.8 us -> 9.76 us  [shards(): pl.pallas_call(target_kernel, out_shape=f32(slots, LANES), in_specs=[VMEM...]
where the time goes in v4:
time: 50 us; the launch traced here: 49.9 us
  blocking collectives  30.8 us (62%)
  Pallas kernels  19 us (38%)
    all_to_all x1, blocking collectives, shards(): lax.all_to_all(payload.reshape(devices, 1, -1), ('gx', 'gy'), split_axis=...  30.8 us
    pallas_call x1, Pallas kernels, shards(): pl.pallas_call(target_kernel, out_shape=f32(slots, LANES), in_specs=[VMEM...  9.76 us
    pallas_call x1, Pallas kernels, shards(): pl.pallas_call(source_kernel, out_shape=[f32(devices * CHUNK, LANES), f32...  9.28 us

profile of v4, /device:TPU:1, one launch (start us, length us, event | category | flops | bytes accessed | tf_op | source)
XLA Modules:
  0.0 49.9 jit_solution(3712046938962463334)
XLA Ops:
  0.0 9.3 %source.1 = (f32[2176,128]{1,0:T(8,128)S(1)}, f32[4096,128]{1,0:T(8,128)S(1)}, bf16[768,256]{1,0:T(8,128)(2,1)S(1)}) custom-call(f32[2048,128]{1,0:T(8,128)} %bitcast.18, f32[4,4,64,64]{3,2,1,0:T(8,128)} %interp_hbm.1, f32[64,4096]{1,0:T(8,128)} %travel_hbm.1, s32[6144]{0:T(1024)} %bitcast.19, s32[6144]{0:T(1024)} %bitcast.21, s32[48,128]{1,0:T(8,128)} %bitcast.20, ...), custom_call_target="tpu_custom_call" | custom-call | tf_op jit(solution)/shard_map/source/pallas_call | solution.py:342
  9.3 30.8 %all_to_all.5 = f32[128,1,2176]{2,1,0:T(1,128)S(1)} all-to-all(f32[128,1,2176]{2,1,0:T(1,128)S(1)} %bitcast.17), channel_id=1, replica_groups=mesh['gx'=8,'gy'=16] {'gx','gy'}, dimensions={0} | all-to-all | bytes 2228224 | tf_op jit(solution)/shard_map/all_to_all | solution.py:371
  40.1 9.8 %target.1 = f32[2048,128]{1,0:T(8,128)} custom-call(f32[2176,128]{1,0:T(8,128)S(1)} %bitcast.16, f32[4096,128]{1,0:T(8,128)S(1)} %get-tuple-element.9.table_ref, bf16[768,256]{1,0:T(8,128)(2,1)S(1)} %get-tuple-element.10.matrix_ref), custom_call_target="tpu_custom_call" | custom-call | tf_op jit(solution)/shard_map/target/pallas_call | solution.py:374

commit v5 on v4

--- a/solution.py
+++ b/solution.py
@@ -78,12 +78,12 @@
 
 
 def source_kernel(
-    w_hbm, interp_hbm, travel_hbm, entry_hbm, exit_hbm, entry_rows_hbm, exit_rows_hbm,
+    w_hbm, interp_hbm, travel_hbm, entry_hbm, exit_hbm,
     out_ref, table_ref, matrix_ref,
-    w_ref, interp_ref, travel_ref, entry_vmem, exit_vmem, entry_ref, exit_ref, next_ref,
-    wave0, wave1, wave2, rows_scratch, x_ref, merged, sems,
+    w_ref, interp_ref, travel_ref, entry_vmem, exit_vmem,
+    wave0, wave1, wave2, rows_scratch, x_ref, merged, sems, *index_refs,
 ):
-    slots = wave0.shape[0]
+    groups = wave0.shape[0] // LANES
     width = travel_ref.shape[1] // PIECES
 
     def piece(p):
@@ -92,13 +92,14 @@
 
     operands = (
         (interp_hbm, interp_ref),
-        (entry_rows_hbm, entry_vmem),
-        (exit_rows_hbm, exit_vmem),
-        (entry_hbm.at[:slots], entry_ref),
-        (exit_hbm.at[:slots], exit_ref),
-        (entry_hbm.at[slots : 2 * slots], next_ref),
+        (entry_hbm, entry_vmem),
+        (exit_hbm, exit_vmem),
         (w_hbm, w_ref),
     )
+    rows = [(entry_hbm, n) for n in range(groups)] + [(exit_hbm, n) for n in range(groups)]
+    rows += [(entry_hbm, groups + n) for n in range(groups)]
+    operands += tuple((ref.at[pl.ds(n, 1), :], to) for (ref, n), to in zip(rows, index_refs))
+    entry_refs, exit_refs, next_refs = [index_refs[n * groups : (n + 1) * groups] for n in range(3)]
     copies = [
         pltpu.make_async_copy(*pair, sems.at[PIECES + n]) for n, pair in enumerate(operands)
     ]
@@ -146,21 +147,20 @@
             table_ref[pl.ds(at, 2 * LANES), :] = jnp.concatenate([cos_part, sin_part], 0).T
             return carry
 
-        return lax.fori_loop(0, width // (2 * LANES), block, carry)
+        return lax.fori_loop(0, width // (2 * LANES), block, carry, unroll=2)
 
     lax.fori_loop(0, PIECES, build, 0)
     for copy in copies[3:]:
         copy.wait()
 
-    size = 64
-
     def gather(step, carry):
-        at = step * size
-        for n in range(size):
-            wave0[pl.ds(at + n, 1), :] = table_ref[pl.ds(entry_ref[at + n], 1), :]
+        for n in range(4):
+            at = step * 4 + n
+            for group in range(groups):
+                wave0[pl.ds(group * LANES + at, 1), :] = table_ref[pl.ds(entry_refs[group][0, at], 1), :]
         return carry
 
-    lax.fori_loop(0, slots // size, gather, 0)
+    lax.fori_loop(0, LANES // 4, gather, 0)
 
     count = tiles * LANES
 
@@ -174,10 +174,12 @@
         chunks = iter(range(8))
 
         def between():
-            base = tile * 4 * LANES + next(chunks) * HALF
-            for n in range(HALF):
-                wave1[pl.ds(base + n, 1), :] = table_ref[pl.ds(exit_ref[base + n], 1), :]
-                wave2[pl.ds(base + n, 1), :] = table_ref[pl.ds(next_ref[base + n], 1), :]
+            base = tile * (LANES // tiles) + next(chunks) * (LANES // tiles // 8)
+            for n in range(LANES // tiles // 8):
+                at = base + n
+                for wave, refs in ((wave1, exit_refs), (wave2, next_refs)):
+                    for group in range(groups):
+                        wave[pl.ds(group * LANES + at, 1), :] = table_ref[pl.ds(refs[group][0, at], 1), :]
 
         for cx in range(2):
             parts = []
@@ -338,7 +340,7 @@
     f32 = lambda *shape: jax.ShapeDtypeStruct(shape, jnp.float32)
     vmem = lambda *shape: pltpu.VMEM(shape, jnp.float32)
     params = pltpu.CompilerParams(vmem_limit_bytes=28 << 20)
-    operands = state, interp, travel, entry_rows.reshape(-1), exit_rows.reshape(-1), entry, exits
+    operands = state, interp, travel, entry, exits
     payload, table, matrix = pl.pallas_call(
         source_kernel,
         out_shape=[
@@ -346,7 +348,7 @@
             f32(travel.shape[1], LANES),
             jax.ShapeDtypeStruct((3 * WIDE, WIDE), jnp.bfloat16),
         ],
-        in_specs=[HBM] * 7,
+        in_specs=[HBM] * 5,
         out_specs=[VMEM] * 3,
         scratch_shapes=[
             vmem(slots, LANES),
@@ -354,17 +356,15 @@
             vmem(*travel.shape),
             pltpu.VMEM(entry.shape, jnp.int32),
             pltpu.VMEM(exits.shape, jnp.int32),
-            pltpu.SMEM((slots,), jnp.int32),
-            pltpu.SMEM((slots,), jnp.int32),
-            pltpu.SMEM((slots,), jnp.int32),
             vmem(slots, LANES),
             vmem(slots, LANES),
             vmem(slots, LANES),
             vmem(count, LANES),
             pltpu.VMEM((WIDE, 3 * WIDE), jnp.bfloat16),
             vmem(slots // 2, WIDE),
-            pltpu.SemaphoreType.DMA((PIECES + 7,)),
-        ],
+            pltpu.SemaphoreType.DMA((PIECES + 4 + 48,)),
+        ]
+        + [pltpu.SMEM((1, LANES), jnp.int32)] * 48,
         compiler_params=params,
         name="source",
     )(*[pltpu.with_memory_space_constraint(x, pltpu.HBM) for x in operands])

time: 50 us -> 49.3 us (0.986)
  Pallas kernels: 19 us -> 18.4 us
    pallas_call x1, Pallas kernels: 9.28 us -> 8.63 us  [shards(): pl.pallas_call(source_kernel, out_shape=[f32(devices * CHUNK, LANES), f32...]
where the time goes in v5:
time: 49.3 us; the launch traced here: 49.2 us
  blocking collectives  30.8 us (62%)
  Pallas kernels  18.4 us (37%)
    all_to_all x1, blocking collectives, shards(): lax.all_to_all(payload.reshape(devices, 1, -1), ('gx', 'gy'), split_axis=...  30.8 us
    pallas_call x1, Pallas kernels, shards(): pl.pallas_call(target_kernel, out_shape=f32(slots, LANES), in_specs=[VMEM...  9.76 us
    pallas_call x1, Pallas kernels, shards(): pl.pallas_call(source_kernel, out_shape=[f32(devices * CHUNK, LANES), f32...  8.63 us

profile of v5, /device:TPU:1, one launch (start us, length us, event | category | flops | bytes accessed | tf_op | source)
XLA Modules:
  0.0 49.2 jit_solution(16853076672455683425)
XLA Ops:
  0.0 8.6 %source.1 = (f32[2176,128]{1,0:T(8,128)S(1)}, f32[4096,128]{1,0:T(8,128)S(1)}, bf16[768,256]{1,0:T(8,128)(2,1)S(1)}) custom-call(f32[2048,128]{1,0:T(8,128)} %bitcast.16, f32[4,4,64,64]{3,2,1,0:T(8,128)} %interp_hbm.1, f32[64,4096]{1,0:T(8,128)} %travel_hbm.1, s32[48,128]{1,0:T(8,128)} %bitcast.17, s32[48,128]{1,0:T(8,128)} %bitcast.18), custom_call_target="tpu_custom_call" | custom-call | tf_op jit(solution)/shard_map/source/pallas_call | solution.py:344
  8.6 30.8 %all_to_all.5 = f32[128,1,2176]{2,1,0:T(1,128)S(1)} all-to-all(f32[128,1,2176]{2,1,0:T(1,128)S(1)} %bitcast.15), channel_id=1, replica_groups=mesh['gx'=8,'gy'=16] {'gx','gy'}, dimensions={0} | all-to-all | bytes 2228224 | tf_op jit(solution)/shard_map/all_to_all | solution.py:371
  39.4 9.8 %target.1 = f32[2048,128]{1,0:T(8,128)} custom-call(f32[2176,128]{1,0:T(8,128)S(1)} %bitcast.14, f32[4096,128]{1,0:T(8,128)S(1)} %get-tuple-element.9.table_ref, bf16[768,256]{1,0:T(8,128)(2,1)S(1)} %get-tuple-element.10.matrix_ref), custom_call_target="tpu_custom_call" | custom-call | tf_op jit(solution)/shard_map/target/pallas_call | solution.py:374

commit v6 on v5

--- a/solution.py
+++ b/solution.py
@@ -243,9 +243,16 @@
                     put(x1_ref, group, i0, jnp.concatenate(rows, 0))
         return carry
 
-    lax.fori_loop(0, 4, first, 0)
-
-    merged[:512, :] = dot(x1_ref.at[:512, :], matrix_ref)
+    lax.fori_loop(0, 2, first, 0, unroll=2)
+    steps = iter((2, 3))
+
+    def rest():
+        for step in steps:
+            first(jnp.int32(step), 0)
+            break
+
+
+    merged[:512, :] = dot(x1_ref.at[:512, :], matrix_ref, rest)
     for copy in copies:
         copy.wait()
 

time: 49.3 us -> 49.2 us (level)
  no operation moved by 1% of the time
where the time goes in v6:
time: 49.2 us; the launch traced here: 49 us
  blocking collectives  30.8 us (63%)
  Pallas kernels  18.2 us (37%)
    all_to_all x1, blocking collectives, shards(): lax.all_to_all(payload.reshape(devices, 1, -1), ('gx', 'gy'), split_axis=...  30.8 us
    pallas_call x1, Pallas kernels, shards(): pl.pallas_call(target_kernel, out_shape=f32(slots, LANES), in_specs=[VMEM...  9.6 us
    pallas_call x1, Pallas kernels, shards(): pl.pallas_call(source_kernel, out_shape=[f32(devices * CHUNK, LANES), f32...  8.64 us

profile of v6, /device:TPU:1, one launch (start us, length us, event | category | flops | bytes accessed | tf_op | source)
XLA Modules:
  0.0 49.0 jit_solution(6199693131248942074)
XLA Ops:
  0.0 8.6 %source.1 = (f32[2176,128]{1,0:T(8,128)S(1)}, f32[4096,128]{1,0:T(8,128)S(1)}, bf16[768,256]{1,0:T(8,128)(2,1)S(1)}) custom-call(f32[2048,128]{1,0:T(8,128)} %bitcast.16, f32[4,4,64,64]{3,2,1,0:T(8,128)} %interp_hbm.1, f32[64,4096]{1,0:T(8,128)} %travel_hbm.1, s32[48,128]{1,0:T(8,128)} %bitcast.17, s32[48,128]{1,0:T(8,128)} %bitcast.18), custom_call_target="tpu_custom_call" | custom-call | tf_op jit(solution)/shard_map/source/pallas_call | solution.py:351
  8.6 30.8 %all_to_all.5 = f32[128,1,2176]{2,1,0:T(1,128)S(1)} all-to-all(f32[128,1,2176]{2,1,0:T(1,128)S(1)} %bitcast.15), channel_id=1, replica_groups=mesh['gx'=8,'gy'=16] {'gx','gy'}, dimensions={0} | all-to-all | bytes 2228224 | tf_op jit(solution)/shard_map/all_to_all | solution.py:378
  39.4 9.6 %target.1 = f32[2048,128]{1,0:T(8,128)} custom-call(f32[2176,128]{1,0:T(8,128)S(1)} %bitcast.14, f32[4096,128]{1,0:T(8,128)S(1)} %get-tuple-element.9.table_ref, bf16[768,256]{1,0:T(8,128)(2,1)S(1)} %get-tuple-element.10.matrix_ref), custom_call_target="tpu_custom_call" | custom-call | tf_op jit(solution)/shard_map/target/pallas_call | solution.py:381
